TPU v7x, 32 devices: a whole 2x2x4 slice. The times are simulated.
32 devices in a mesh: dp: 32 (over z, y, x, core).
Axes of the slice: x: 2, y: 2, z: 4, core: 2. Of those that a mesh axis runs over, the one named last changes fastest.
Arguments:
- features: bfloat16 [64, 256, 256], P('dp'), may hold values from -6 to 6
- frame_lens: int32 [64], P('dp'), may hold values from 128 to 256
- labels: int32 [64, 48], P('dp'), may hold values from 1 to 255
- label_lens: int32 [64], P('dp'), may hold values from 1 to 48
- w_up: float32 [262144], P('dp'), may hold values from -0.375 to 0.375
- w_down: float32 [262144], P('dp'), may hold values from -0.1875 to 0.1875
- w_out: float32 [65536], P('dp'), may hold values from -1.125 to 1.125
- first_up: float32 [262144], P('dp'), may hold values from -0.00018 to 0.00018
- first_down: float32 [262144], P('dp'), may hold values from -0.00018 to 0.00018
- first_out: float32 [65536], P('dp'), may hold values from -0.00018 to 0.00018
- second_up: float32 [262144], P('dp'), may hold values from 1e-10 to 1e-08
- second_down: float32 [262144], P('dp'), may hold values from 1e-10 to 1e-08
- second_out: float32 [65536], P('dp'), may hold values from 1e-10 to 1e-08
Outputs:
- new_up: float32 [262144], P('dp')
- new_down: float32 [262144], P('dp')
- new_out: float32 [65536], P('dp')
- new_first_up: float32 [262144], P('dp')
- new_first_down: float32 [262144], P('dp')
- new_first_out: float32 [65536], P('dp')
- new_second_up: float32 [262144], P('dp')
- new_second_down: float32 [262144], P('dp')
- new_second_out: float32 [65536], P('dp')
Inputs may be any that keep to these rules, and one draw needn't show every extreme that they name: `labels`: 0 is the blank and is not a label.
All inputs are finite; a program needn't handle non-finite values.
Results may differ from a plain program's by a relative error of at most 0.002.
The roundings to bfloat16 on the way count: a program that leaves them out, or rounds other values in their place, can miss the bound.
Values may be sent and summed in bfloat16 or wider, within the bound.
A program may use at most 64 MiB of HBM per device.

v0:
```python
import functools

import jax
import jax.numpy as jnp
from jax import lax
from jax.experimental import pallas as pl
from jax.experimental.pallas import tpu as pltpu
from jax.sharding import PartitionSpec as P

D = 256
FF = 1024
VOCAB = 256
LANES = 128
MESH = pl.DeviceIdType.MESH

first_correction = 1.0 - (0.9**10) ** 10
second_correction = 1.0 - (0.999**10) ** 10
negative = -1e30
VMEM = pl.BlockSpec(memory_space=pltpu.VMEM)
SMEM = pl.BlockSpec(memory_space=pltpu.SMEM)
HBM = pl.BlockSpec(memory_space=pltpu.HBM)


def flip(me, bit):
    return me + bit - 2 * bit * ((me // bit) % 2)


def bit_orders(devices):
    bits = [1 << k for k in range(devices.bit_length() - 1)]
    core, rest = bits[:1], bits[1:]
    down = rest[::-1]
    swapped = down[:-2] + down[-2:][::-1]
    turned = down[-2:] + down[:-2]
    return (down + core, swapped + core, turned + core)


def subsets(bits):
    offsets = [0]
    for bit in bits:
        offsets = offsets + [offset + bit for offset in offsets]
    return offsets


def place_with(me, free, pattern):
    place = me
    for bit in free:
        if pattern & bit:
            place = flip(place, bit)
    return place


class Gather:
    def __init__(self, me, devices, fulls, send_sem, recv_sem):
        self.me, self.fulls = me, fulls
        self.send_sem, self.recv_sem = send_sem, recv_sem
        self.orders = bit_orders(devices)
        self.steps = len(self.orders[0])
        self.copies = [{}, {}, {}]

    def fill(self, shards):
        for shard, full in zip(shards, self.fulls):
            rows, width = full.shape[1:]
            parts = width // LANES
            for part in range(parts):
                full[self.me, :, part * LANES : (part + 1) * LANES] = shard[
                    pl.ds(part, rows, stride=parts), :
                ].astype(jnp.bfloat16)

    def send(self, which, pattern, stage):
        order, full = self.orders[which], self.fulls[which]
        owner = place_with(self.me, order[:stage], pattern)
        slot = pattern + order[stage]
        copy = pltpu.make_async_remote_copy(
            src_ref=full.at[owner],
            dst_ref=full.at[owner],
            send_sem=self.send_sem.at[which, slot],
            recv_sem=self.recv_sem.at[which, slot],
            device_id=(flip(self.me, order[stage]),),
            device_id_type=MESH,
        )
        copy.start()
        self.copies[which][slot] = copy

    def pass_on(self):
        for which in range(3):
            for stage in range(self.steps):
                self.send(which, 0, stage)
        for stage in range(self.steps - 1):
            for at in range(1 << stage):
                for which in range(3):
                    order = self.orders[which]
                    pattern = subsets(order[:stage])[at] + order[stage]
                    self.copies[which][pattern].wait_recv()
                    for later in range(stage + 1, self.steps):
                        self.send(which, pattern, later)

    def arrive(self, which):
        order = self.orders[which]
        for pattern in subsets(order[:-1]):
            self.copies[which][pattern + order[-1]].wait_recv()

    def close(self):
        for copies in self.copies:
            for copy in copies.values():
                copy.wait_send()


def greet(me, devices, barrier):
    @pl.loop(1, devices)
    def _(shift):
        pl.semaphore_signal(
            barrier, inc=1, device_id=((me + shift) % devices,), device_id_type=MESH
        )


def gather_kernel(devices, w_up, w_down, w_out, full_up, full_down, full_out, send_sem, recv_sem):
    me = lax.axis_index("dp")
    barrier = pltpu.get_barrier_semaphore()
    greet(me, devices, barrier)
    gather = Gather(me, devices, (full_up, full_down, full_out), send_sem, recv_sem)
    gather.fill((w_up, w_down, w_out))
    pl.semaphore_wait(barrier, devices - 1)
    gather.pass_on()
    for which in range(3):
        gather.arrive(which)
    gather.close()


def gather_weights(devices, w_up, w_down, w_out):
    shapes = []
    for shard, width in ((w_up, FF), (w_down, D), (w_out, VOCAB)):
        shapes.append(
            jax.ShapeDtypeStruct((devices, shard.size // width, width), jnp.bfloat16)
        )
    return pl.pallas_call(
        functools.partial(gather_kernel, devices),
        out_shape=shapes,
        in_specs=[VMEM] * 3,
        out_specs=[VMEM] * 3,
        scratch_shapes=[
            pltpu.SemaphoreType.DMA((3, devices)),
            pltpu.SemaphoreType.DMA((3, devices)),
        ],
        compiler_params=pltpu.CompilerParams(collective_id=0, has_side_effects=True),
        name="gather_weights",
    )(w_up, w_down, w_out)


def dot_rows(left, right):
    return jnp.dot(left, right, preferred_element_type=jnp.float32)


def dot_last(left, right, precision=None):
    return lax.dot_general(
        left, right, (((1,), (1,)), ((), ())), precision=precision,
        preferred_element_type=jnp.float32,
    )


def dot_first(left, right):
    return lax.dot_general(
        left, right, (((0,), (0,)), ((), ())), preferred_element_type=jnp.float32
    )


def row_blocks(total, body):
    block = min(128, total)

    @pl.loop(0, total // block)
    def _(step):
        body(pl.ds(pl.multiple_of(step * block, block), block))


def normalize(features, normalized):
    def body(rows):
        flat_in = features[rows, :].astype(jnp.float32)
        centre = jnp.mean(flat_in, axis=1, keepdims=True)
        shifted = flat_in - centre
        spread = jnp.mean(shifted * shifted, axis=1, keepdims=True)
        normalized[rows, :] = (shifted * lax.rsqrt(spread + 1e-05)).astype(jnp.bfloat16)

    row_blocks(features.shape[0], body)


def project_up(normalized, up_mat, activation, hidden):
    def body(rows):
        act = dot_rows(normalized[rows, :], up_mat[...].reshape(D, FF))
        activation[rows, :] = act
        hidden[rows, :] = (act * (1.0 / (1.0 + jnp.exp(-act)))).astype(jnp.bfloat16)

    row_blocks(normalized.shape[0], body)


def project_down(features, hidden, down_mat, out_mat, block_out, log_probs):
    def body(rows):
        flat_in = features[rows, :].astype(jnp.float32)
        out_rows = (flat_in + 0.5 * dot_rows(hidden[rows, :], down_mat[...].reshape(FF, D))).astype(
            jnp.bfloat16
        )
        block_out[rows, :] = out_rows
        logits = dot_rows(out_rows, out_mat[...].reshape(D, VOCAB))
        top = jnp.max(logits, axis=1, keepdims=True)
        low = logits - top
        log_probs[rows, :] = low - jnp.log(jnp.sum(jnp.exp(low), axis=1, keepdims=True))

    row_blocks(features.shape[0], body)


def ctc_grad(
    loss_scale,
    frame_lens,
    label_lens,
    labels,
    log_probs,
    emitted,
    alpha_rows,
    beta_rows,
    logit_grad,
):
    utterances, label_count = labels.shape
    frames = log_probs.shape[0] // utterances
    states = 2 * label_count + 1

    label_ids = lax.broadcasted_iota(jnp.int32, (label_count, LANES), 0)
    state_at = lax.broadcasted_iota(jnp.int32, (label_count, LANES), 1)
    spread_now = (state_at == 2 * label_ids + 1).astype(jnp.bfloat16)
    spread_back = (state_at == 2 * label_ids + 3).astype(jnp.bfloat16)
    spread_ahead = (state_at == 2 * label_ids - 1).astype(jnp.bfloat16)
    label_rows = jnp.concatenate(
        [
            labels[...].astype(jnp.float32),
            jnp.zeros((8 - utterances, label_count), jnp.float32),
        ],
        axis=0,
    ).astype(jnp.bfloat16)
    extended = dot_rows(label_rows, spread_now)
    earlier = dot_rows(label_rows, spread_back)
    later = dot_rows(label_rows, spread_ahead)
    row_ids = lax.broadcasted_iota(jnp.int32, (8, LANES), 0)
    lane_ids = lax.broadcasted_iota(jnp.int32, (8, LANES), 1)
    may_skip = (extended > 0.5) & (extended != earlier)
    skip_later = (later > 0.5) & (later != extended)
    skip_add = jnp.where(may_skip, 0.0, negative)
    later_add = jnp.where(skip_later, 0.0, negative)
    ends = jnp.full((8, LANES), -9, jnp.int32)
    first_frame = jnp.full((8, LANES), -9, jnp.int32)
    for utterance in range(utterances):
        ends = jnp.where(row_ids == utterance, 2 * label_lens[utterance], ends)
        first_frame = jnp.where(row_ids == utterance, frame_lens[utterance] - 1, first_frame)
    finish = jnp.where((lane_ids == ends) | (lane_ids == ends - 1), 0.0, negative)

    emitted[...] = jnp.full(emitted.shape, negative, jnp.float32)
    vocab_ids = lax.broadcasted_iota(jnp.int32, (VOCAB, LANES), 0).astype(jnp.float32)
    lanes_wide = lax.broadcasted_iota(jnp.int32, (VOCAB, LANES), 1)
    frame_lanes = lax.broadcasted_iota(jnp.int32, (frames, LANES), 1)
    onehots = []
    for utterance in range(utterances):
        onehot = jnp.where(
            (vocab_ids == extended[utterance : utterance + 1, :]) & (lanes_wide < states), 1.0, 0.0
        )
        onehots.append(onehot)
        picked = jnp.dot(
            log_probs[utterance * frames : (utterance + 1) * frames, :],
            onehot,
            precision=lax.Precision.HIGHEST,
            preferred_element_type=jnp.float32,
        )
        emitted[:, utterance, :] = jnp.where(frame_lanes < states, picked, negative)

    def log_three(one, two, three):
        top = jnp.maximum(jnp.maximum(one, two), three)
        return top + jnp.log(jnp.exp(one - top) + jnp.exp(two - top) + jnp.exp(three - top))

    def ahead(values, count):
        return pltpu.roll(values, count, 1) if count else values

    def behind(values, count):
        return pltpu.roll(values, LANES - count, 1) if count else values

    skips = [ahead(skip_add, count) for count in range(3)]
    later_skips = [behind(later_add, count) for count in range(3)]
    finishes = [behind(finish, count) for count in range(3)]

    def advance(pair, carry):
        alpha, weighted = carry
        frame = 2 * pair
        back = frames - 1 - frame
        moved = [ahead(alpha, count) for count in range(5)]
        other = [behind(weighted, count) for count in range(5)]
        emit, emit_back = emitted[frame], emitted[back]
        ends_here = first_frame == back
        firsts, lasts = [], []
        for count in range(3):
            base = log_three(moved[count], moved[count + 1], moved[count + 2] + skips[count])
            rest = log_three(other[count], other[count + 1], other[count + 2] + later_skips[count])
            rest = jnp.where(ends_here, finishes[count], rest)
            if count == 0:
                alpha_rows[frame] = base
                beta_rows[back] = rest
            firsts.append(base + ahead(emit, count))
            lasts.append(rest + behind(emit_back, count))
        base = log_three(firsts[0], firsts[1], firsts[2] + skips[0])
        rest = log_three(lasts[0], lasts[1], lasts[2] + later_skips[0])
        rest = jnp.where(first_frame == back - 1, finish, rest)
        alpha_rows[frame + 1] = base
        beta_rows[back - 1] = rest
        return (base + emitted[frame + 1], rest + emitted[back - 1])

    nothing = jnp.full((8, LANES), negative, jnp.float32)
    start = jnp.where(lane_ids == 0, 0.0, negative)
    lax.fori_loop(0, frames // 2, advance, (start, nothing), unroll=8)

    frame_ids = lax.broadcasted_iota(jnp.int32, (frames, LANES), 0)
    for utterance in range(utterances):
        joint = (
            alpha_rows[:, utterance, :] + emitted[:, utterance, :] + beta_rows[:, utterance, :]
        )
        top = jnp.max(joint, axis=1, keepdims=True)
        mass = jnp.exp(joint - top)
        share = mass / jnp.sum(mass, axis=1, keepdims=True)
        occupancy = jnp.where(frame_ids < frame_lens[utterance], share, 0.0)
        gamma = dot_last(occupancy, onehots[utterance], lax.Precision.HIGHEST)
        rows = slice(utterance * frames, (utterance + 1) * frames)
        probs = jnp.exp(log_probs[rows, :])
        held = jnp.sum(occupancy, axis=1, keepdims=True)
        logit_grad[rows, :] = (loss_scale * (probs * held - gamma)).astype(jnp.bfloat16)


def grad_ff(logit_grad, out_mat, ff_grad):
    def body(rows):
        ff_grad[rows, :] = (
            0.5 * dot_last(logit_grad[rows, :], out_mat[...].reshape(D, VOCAB))
        ).astype(jnp.bfloat16)

    row_blocks(logit_grad.shape[0], body)


def grad_act(ff_grad, down_mat, activation, act_grad):
    def body(rows):
        act = activation[rows, :]
        sigmoid = 1.0 / (1.0 + jnp.exp(-act))
        slope = sigmoid * (1.0 + act * (1.0 - sigmoid))
        act_grad[rows, :] = (
            dot_last(ff_grad[rows, :], down_mat[...].reshape(FF, D)) * slope
        ).astype(jnp.bfloat16)

    row_blocks(ff_grad.shape[0], body)


def step_kernel(
    loss_scale,
    frame_lens,
    label_lens,
    features,
    labels,
    up_mat,
    down_mat,
    out_mat,
    grad_up,
    grad_down,
    grad_out,
    normalized,
    activation,
    hidden,
    block_out,
    log_probs,
    emitted,
    alpha_rows,
    beta_rows,
    logit_grad,
    ff_grad,
    act_grad,
):
    normalize(features, normalized)
    project_up(normalized, up_mat, activation, hidden)
    project_down(features, hidden, down_mat, out_mat, block_out, log_probs)
    ctc_grad(
        loss_scale, frame_lens, label_lens, labels, log_probs, emitted, alpha_rows, beta_rows,
        logit_grad,
    )
    grad_ff(logit_grad, out_mat, ff_grad)
    grad_act(ff_grad, down_mat, activation, act_grad)
    grad_up[...] = dot_first(normalized[...], act_grad[...])
    grad_down[...] = dot_first(hidden[...], ff_grad[...])
    grad_out[...] = dot_first(block_out[...], logit_grad[...])


def step_scratch(total, frames):
    return [
        pltpu.VMEM((total, D), jnp.bfloat16),
        pltpu.VMEM((total, FF), jnp.float32),
        pltpu.VMEM((total, FF), jnp.bfloat16),
        pltpu.VMEM((total, D), jnp.bfloat16),
        pltpu.VMEM((total, VOCAB), jnp.float32),
        pltpu.VMEM((frames, 8, LANES), jnp.float32),
        pltpu.VMEM((frames, 8, LANES), jnp.float32),
        pltpu.VMEM((frames, 8, LANES), jnp.float32),
        pltpu.VMEM((total, VOCAB), jnp.bfloat16),
        pltpu.VMEM((total, D), jnp.bfloat16),
        pltpu.VMEM((total, FF), jnp.bfloat16),
    ]


def local_step(loss_scale, frame_lens, label_lens, features, labels, up_mat, down_mat, out_mat):
    total = features.shape[0]
    frames = total // labels.shape[0]
    return pl.pallas_call(
        functools.partial(step_kernel, loss_scale),
        out_shape=[
            jax.ShapeDtypeStruct((D, FF), jnp.float32),
            jax.ShapeDtypeStruct((FF, D), jnp.float32),
            jax.ShapeDtypeStruct((D, VOCAB), jnp.float32),
        ],
        in_specs=[SMEM, SMEM] + [VMEM] * 5,
        out_specs=[VMEM] * 3,
        scratch_shapes=step_scratch(total, frames),
        compiler_params=pltpu.CompilerParams(vmem_limit_bytes=40 << 20),
        name="local_step",
    )(frame_lens, label_lens, features, labels, up_mat, down_mat, out_mat)


class Sum:
    def __init__(self, me, devices, grads, received, staged, send_sem, recv_sem):
        self.me, self.grads, self.received, self.staged = me, grads, received, staged
        self.send_sem, self.recv_sem = send_sem, recv_sem
        self.orders = [order[::-1] for order in bit_orders(devices)]
        self.steps = len(self.orders[0])
        self.copies = [{}, {}, {}]

    def sum_of(self, which, place, pattern, stage):
        value = self.grads[which][place]
        for bit in self.orders[which][:stage]:
            self.copies[which][pattern + bit].wait_recv()
            value = value + self.received[which][pattern + bit]
        return value

    def send(self, which, stage):
        order = self.orders[which]
        for offset in subsets(order[stage + 1 :][::-1])[::-1]:
            slot = offset + order[stage]
            place = place_with(self.me, order, slot)
            if stage == 0:
                source = self.grads[which].at[place]
            else:
                self.staged[which][slot] = self.sum_of(which, place, slot, stage)
                source = self.staged[which].at[slot]
            copy = pltpu.make_async_remote_copy(
                src_ref=source,
                dst_ref=self.received[which].at[slot],
                send_sem=self.send_sem.at[which, slot],
                recv_sem=self.recv_sem.at[which, slot],
                device_id=(flip(self.me, order[stage]),),
                device_id_type=MESH,
            )
            copy.start()
            self.copies[which][slot] = copy

    def finish(self, devices, reduced, squares, own_squares, small_send, small_recv):
        me = self.me
        own = jnp.zeros((1, LANES), jnp.float32)
        for which in (2, 1, 0):
            value = self.sum_of(which, me, 0, self.steps)
            rows, width = value.shape
            parts = width // LANES
            for part in range(parts):
                piece = value[:, part * LANES : (part + 1) * LANES]
                reduced[which][pl.ds(part, rows, stride=parts), :] = piece
                own = own + jnp.sum(piece * piece, axis=0, keepdims=True)
        own_squares[...] = own
        squares[0] = own

        def small_copy(shift):
            return pltpu.make_async_remote_copy(
                src_ref=own_squares,
                dst_ref=squares.at[shift],
                send_sem=small_send.at[shift],
                recv_sem=small_recv.at[shift],
                device_id=((me + shift) % devices,),
                device_id_type=MESH,
            )

        @pl.loop(1, devices)
        def _(shift):
            small_copy(shift).start()

        for copies in self.copies:
            for copy in copies.values():
                copy.wait_send()

        @pl.loop(1, devices)
        def _(shift):
            small_copy(shift).wait()


def sum_kernel(devices, *refs):
    grads, reduced, squares = refs[:3], refs[3:6], refs[6]
    received, staged = refs[7:10], refs[10:13]
    own_squares, send_sem, recv_sem, small_send, small_recv = refs[13:]
    me = lax.axis_index("dp")
    barrier = pltpu.get_barrier_semaphore()
    greet(me, devices, barrier)
    pl.semaphore_wait(barrier, devices - 1)
    total = Sum(me, devices, grads, received, staged, send_sem, recv_sem)
    for stage in range(total.steps):
        for which in range(3):
            total.send(which, stage)
    total.finish(devices, reduced, squares, own_squares, small_send, small_recv)


def fused_kernel(devices, loss_scale, *refs):
    frame_lens, label_lens, features, labels = refs[:4]
    shards, reduced, squares = refs[4:7], refs[7:10], refs[10]
    fulls, grads, received, staged = refs[11:14], refs[14:17], refs[17:20], refs[20:23]
    gather_send, gather_recv, own_squares, send_sem, recv_sem, small_send, small_recv = refs[23:30]
    normalized, activation, hidden, block_out, log_probs = refs[30:35]
    emitted, alpha_rows, beta_rows, logit_grad, ff_grad, act_grad = refs[35:41]
    held, load_sem = refs[41:45], refs[45]
    up_mat, down_mat, out_mat = fulls
    me = lax.axis_index("dp")
    loads = [
        pltpu.make_async_copy(source, target, load_sem.at[at])
        for at, (source, target) in enumerate(zip((*shards, features), held))
    ]
    for load in loads:
        load.start()
    shards, features = held[:3], held[3]
    barrier = pltpu.get_barrier_semaphore()
    greet(me, devices, barrier)
    gather = Gather(me, devices, fulls, gather_send, gather_recv)
    for load in loads[:3]:
        load.wait()
    gather.fill(shards)
    loads[3].wait()
    normalize(features, normalized)
    pl.semaphore_wait(barrier, devices - 1)
    gather.pass_on()
    gather.arrive(0)
    project_up(normalized, up_mat, activation, hidden)
    gather.arrive(1)
    gather.arrive(2)
    project_down(features, hidden, down_mat, out_mat, block_out, log_probs)
    ctc_grad(
        loss_scale, frame_lens, label_lens, labels, log_probs, emitted, alpha_rows, beta_rows,
        logit_grad,
    )
    total = Sum(me, devices, grads, received, staged, send_sem, recv_sem)
    pending = [list(range(total.steps)) for _ in range(3)]

    def advance(*whiches):
        for which in whiches:
            if pending[which]:
                total.send(which, pending[which].pop(0))

    def put(which, value):
        grads[which][...] = value.reshape(grads[which].shape)

    grad_ff(logit_grad, out_mat, ff_grad)
    put(1, dot_first(hidden[...], ff_grad[...]))
    advance(1)
    grad_act(ff_grad, down_mat, activation, act_grad)
    advance(1)
    put(0, dot_first(normalized[...], act_grad[...]))
    advance(0)
    put(2, dot_first(block_out[...], logit_grad[...]))
    advance(2)
    while any(pending):
        advance(1, 0, 2)
    total.finish(devices, reduced, squares, own_squares, small_send, small_recv)
    gather.close()


def fused_step(loss_scale, devices, frame_lens, label_lens, features, labels, weights):
    total = features.shape[0]
    frames = total // labels.shape[0]
    blocks = [
        (devices, weight.size // width, width)
        for weight, width in zip(weights, (FF, D, VOCAB))
    ]
    wide = [pltpu.VMEM(block, jnp.float32) for block in blocks]
    return pl.pallas_call(
        functools.partial(fused_kernel, devices, loss_scale),
        out_shape=[jax.ShapeDtypeStruct(weight.shape, jnp.float32) for weight in weights]
        + [jax.ShapeDtypeStruct((devices, 1, LANES), jnp.float32)],
        in_specs=[SMEM, SMEM, HBM, VMEM] + [HBM] * 3,
        out_specs=[VMEM] * 4,
        scratch_shapes=[pltpu.VMEM(block, jnp.bfloat16) for block in blocks]
        + wide * 3
        + [
            pltpu.SemaphoreType.DMA((3, devices)),
            pltpu.SemaphoreType.DMA((3, devices)),
            pltpu.VMEM((1, LANES), jnp.float32),
            pltpu.SemaphoreType.DMA((3, devices)),
            pltpu.SemaphoreType.DMA((3, devices)),
            pltpu.SemaphoreType.DMA((devices,)),
            pltpu.SemaphoreType.DMA((devices,)),
        ]
        + step_scratch(total, frames)
        + [pltpu.VMEM(array.shape, array.dtype) for array in (*weights, features)]
        + [pltpu.SemaphoreType.DMA((4,))],
        compiler_params=pltpu.CompilerParams(
            collective_id=2, has_side_effects=True, vmem_limit_bytes=67043328
        ),
        name="fused_step",
    )(frame_lens, label_lens, features, labels, *weights)


def sum_gradients(devices, grads):
    blocks = [grad.reshape(devices, grad.shape[0] // devices, grad.shape[1]) for grad in grads]
    shapes = [
        jax.ShapeDtypeStruct((block[0].size // LANES, LANES), jnp.float32) for block in blocks
    ]
    buffers = [pltpu.VMEM(block.shape, jnp.float32) for block in blocks]
    return pl.pallas_call(
        functools.partial(sum_kernel, devices),
        out_shape=shapes + [jax.ShapeDtypeStruct((devices, 1, LANES), jnp.float32)],
        in_specs=[VMEM] * 3,
        out_specs=[VMEM] * 4,
        scratch_shapes=buffers
        + buffers
        + [
            pltpu.VMEM((1, LANES), jnp.float32),
            pltpu.SemaphoreType.DMA((3, devices)),
            pltpu.SemaphoreType.DMA((3, devices)),
            pltpu.SemaphoreType.DMA((devices,)),
            pltpu.SemaphoreType.DMA((devices,)),
        ],
        compiler_params=pltpu.CompilerParams(
            collective_id=1, has_side_effects=True, vmem_limit_bytes=50 << 20
        ),
        name="sum_gradients",
    )(*blocks)


def adam_kernel(squares, *refs):
    weights, firsts, seconds, grads, outs = (refs[at : at + 3] for at in (0, 3, 6, 9, 12))
    new_firsts, new_seconds = refs[15:18], refs[18:21]
    total = jnp.sum(squares[...])
    clip = 1.0 / jnp.maximum(jnp.sqrt(jnp.full((1, LANES), total)), 1.0)
    for which in range(3):
        scaled = clip * grads[which][...]
        first = 0.9 * firsts[which][...] + 0.1 * scaled
        second = 0.999 * seconds[which][...] + 0.001 * scaled * scaled
        ratio = first / first_correction / (jnp.sqrt(second / second_correction) + 1e-08)
        outs[which][...] = weights[which][...] - 0.001 * ratio
        new_firsts[which][...] = first
        new_seconds[which][...] = second


def adam(squares, weights, firsts, seconds, grads):
    shapes = [jax.ShapeDtypeStruct(weight.shape, jnp.float32) for weight in weights]
    return pl.pallas_call(
        adam_kernel,
        out_shape=shapes * 3,
        in_specs=[VMEM] * 13,
        out_specs=[VMEM] * 9,
        compiler_params=pltpu.CompilerParams(vmem_limit_bytes=67043328),
        name="adam",
    )(squares, *weights, *firsts, *seconds, *grads)


def per_device(
    features,
    frame_lens,
    labels,
    label_lens,
    w_up,
    w_down,
    w_out,
    first_up,
    first_down,
    first_out,
    second_up,
    second_down,
    second_out,
):
    devices = lax.axis_size("dp")
    batch, frames, width = features.shape

    def lined(*arrays):
        return [array.reshape(array.shape[0] // LANES, LANES) for array in arrays]

    weights = lined(w_up, w_down, w_out)
    loss_scale = 1.0 / (batch * devices)
    rows_in = features.reshape(batch * frames, width)
    if w_up.size % (8 * FF) == 0 and w_out.size % (8 * VOCAB) == 0:
        *shares, squares = fused_step(
            loss_scale, devices, frame_lens, label_lens, rows_in, labels, weights
        )
    else:
        full_up, full_down, full_out = gather_weights(devices, *weights)
        grads = local_step(
            loss_scale,
            frame_lens,
            label_lens,
            rows_in,
            labels,
            full_up.reshape(D, FF),
            full_down.reshape(FF, D),
            full_out.reshape(D, VOCAB),
        )
        *shares, squares = sum_gradients(devices, grads)
    results = adam(
        squares,
        weights,
        lined(first_up, first_down, first_out),
        lined(second_up, second_down, second_out),
        shares,
    )
    return tuple(result.reshape(-1) for result in results)


def solution(mesh):
    flat = P("dp")
    return jax.shard_map(
        per_device,
        mesh=mesh,
        in_specs=(P("dp", None, None), flat, P("dp", None), flat) + (flat,) * 9,
        out_specs=(flat,) * 9,
        check_vma=False,
    )
```

profile of v0, /device:TPU:0, one launch (start us, length us, event | category | flops | bytes accessed | tf_op | source)
XLA Modules:
  0.0 75.2 jit_solution(152096052148345140)
XLA Ops:
  0.6 72.8 %fused_step.1 = (f32[64,128]{1,0:T(8,128)}, f32[64,128]{1,0:T(8,128)}, f32[16,128]{1,0:T(8,128)}, f32[32,1,128]{2,1,0:T(1,128)}) custom-call(s32[2]{0:T(128)} %refs_0_.1, s32[2]{0:T(128)} %refs_1_.1, bf16[512,256]{1,0:T(8,128)(2,1)} %bitcast.19, s32[2,48]{1,0:T(2,128)} %refs_3_.1, f32[64,128]{1,0:T(8,128)} %bitcast.20, f32[64,128]{1,0:T(8,128)} %bitcast.22, ...), custom_call_target="tpu_custom_call" | custom-call | tf_op jit(solution)/shard_map/fused_step/pallas_call | solution.py:580
  73.4 1.8 %adam.1 = (f32[64,128]{1,0:T(8,128)}, f32[64,128]{1,0:T(8,128)}, f32[16,128]{1,0:T(8,128)}, f32[64,128]{1,0:T(8,128)}, f32[64,128]{1,0:T(8,128)}, /*index=5*/f32...) custom-call(f32[32,1,128]{2,1,0:T(1,128)} %get-tuple-element.22.squares, f32[64,128]{1,0:T(8,128)} %bitcast.21, ...), custom_call_target="tpu_custom_call" | custom-call | tf_op jit(solution)/shard_map/adam/pallas_call | solution.py:651
where the time goes:
time: 75.5 us; the launch traced here: 75.2 us
  Pallas kernels  74.6 us (99%)
    pallas_call x1, Pallas kernels, fused_step(): pl.pallas_call(functools.partial(fused_kernel, devices, loss_scale), out_...  72.8 us
    pallas_call x1, Pallas kernels, adam(): pl.pallas_call(adam_kernel, out_shape=shapes * 3, in_specs=[VMEM] * 13, o...  1.81 us

commit v1 on v0

--- a/solution.py
+++ b/solution.py
@@ -103,6 +103,92 @@
         for copies in self.copies:
             for copy in copies.values():
                 copy.wait_send()
+
+
+def drain(ref, blocks, send_sem, recv_sem, peer):
+    return pltpu.make_async_remote_copy(
+        src_ref=ref.at[pl.ds(0, blocks)],
+        dst_ref=ref.at[pl.ds(0, blocks)],
+        send_sem=send_sem,
+        recv_sem=recv_sem,
+        device_id=(peer,),
+        device_id_type=MESH,
+    )
+
+
+class GroupGather:
+    def __init__(self, me, devices, fulls, send_sem, recv_sem):
+        self.me, self.devices, self.fulls = me, devices, fulls
+        self.send_sem, self.recv_sem = send_sem, recv_sem
+        self.orders = bit_orders(devices)
+        self.steps = len(self.orders[0])
+
+    def fill(self, shards):
+        for shard, full in zip(shards, self.fulls):
+            rows, width = full.shape[1:]
+            parts = width // LANES
+            for part in range(parts):
+                full[self.me, :, part * LANES : (part + 1) * LANES] = shard[
+                    pl.ds(part, rows, stride=parts), :
+                ].astype(jnp.bfloat16)
+
+    def sem_at(self, stage, group):
+        return stage * (stage + 1) // 2 + (group if stage < self.steps - 1 else 0)
+
+    def send(self, which, patterns, stage, group):
+        order, full = self.orders[which], self.fulls[which]
+        for pattern in patterns:
+            owner = place_with(self.me, order[:stage], pattern)
+            pltpu.make_async_remote_copy(
+                src_ref=full.at[owner],
+                dst_ref=full.at[owner],
+                send_sem=self.send_sem.at[which],
+                recv_sem=self.recv_sem.at[which, self.sem_at(stage, group)],
+                device_id=(flip(self.me, order[stage]),),
+                device_id_type=MESH,
+            ).start()
+
+    def drain(self, which, blocks, at):
+        return drain(
+            self.fulls[which], blocks, self.send_sem.at[which], self.recv_sem.at[which, at],
+            flip(self.me, 1),
+        )
+
+    def pass_on(self):
+        for which in range(3):
+            for stage in range(self.steps):
+                self.send(which, [0], stage, 0)
+        for stage in range(self.steps - 1):
+            for group in range(stage + 1):
+                for which in range(3):
+                    order = self.orders[which]
+                    patterns = [0]
+                    if group:
+                        patterns = [at + order[group - 1] for at in subsets(order[: group - 1])]
+                    self.drain(which, len(patterns), self.sem_at(stage, group)).wait_recv()
+                    patterns = [pattern + order[stage] for pattern in patterns]
+                    for later in range(stage + 1, self.steps):
+                        self.send(which, patterns, later, stage + 1)
+
+    def arrive(self, which):
+        last = self.steps - 1
+        self.drain(which, 1 << last, self.sem_at(last, 0)).wait_recv()
+
+    def close(self):
+        for which in range(3):
+            self.drain(which, self.devices - 1, 0).wait_send()
+
+
+def gather_sems(devices):
+    steps = devices.bit_length() - 1
+    return (steps - 1) * steps // 2 + 1
+
+
+def greet_partners(me, devices, barrier):
+    for step in range(devices.bit_length() - 1):
+        pl.semaphore_signal(
+            barrier, inc=1, device_id=(flip(me, 1 << step),), device_id_type=MESH
+        )
 
 
 def greet(me, devices, barrier):
@@ -492,6 +578,111 @@
             small_copy(shift).wait()
 
 
+def chunks(blocks):
+    if blocks >= 4:
+        return [blocks // 4, blocks // 4, blocks // 2]
+    return [1] * blocks
+
+
+def sum_groups(steps):
+    groups, sems = [], 0
+    for stage in range(steps):
+        sizes = chunks(1 << (steps - 1 - stage))
+        groups.append((sems, sizes))
+        sems += len(sizes)
+    return groups, sems
+
+
+class GroupSum:
+    def __init__(self, me, devices, grads, received, staged, send_sem, recv_sem):
+        self.me, self.devices = me, devices
+        self.grads, self.received, self.staged = grads, received, staged
+        self.send_sem, self.recv_sem = send_sem, recv_sem
+        self.orders = [order[::-1] for order in bit_orders(devices)]
+        self.steps = len(self.orders[0])
+        self.groups, _ = sum_groups(self.steps)
+        self.seen = set()
+
+    def slots(self, which, stage):
+        order = self.orders[which]
+        return [
+            offset + order[stage] for offset in subsets(order[stage + 1 :][::-1])[::-1]
+        ]
+
+    def sem_at(self, which, stage, slot):
+        at = self.slots(which, stage).index(slot)
+        sem, sizes = self.groups[stage]
+        for size in sizes:
+            if at < size:
+                return sem, size
+            at, sem = at - size, sem + 1
+
+    def sum_of(self, which, place, pattern, stage):
+        value = self.grads[which][place]
+        for at, bit in enumerate(self.orders[which][:stage]):
+            sem, size = self.sem_at(which, at, pattern + bit)
+            if (which, sem) not in self.seen:
+                self.seen.add((which, sem))
+                drain(
+                    self.received[which], size, self.send_sem.at[which],
+                    self.recv_sem.at[which, sem], flip(self.me, bit),
+                ).wait_recv()
+            value = value + self.received[which][pattern + bit]
+        return value
+
+    def send(self, which, stage):
+        order = self.orders[which]
+        for slot in self.slots(which, stage):
+            place = place_with(self.me, order, slot)
+            if stage == 0:
+                source = self.grads[which].at[place]
+            else:
+                self.staged[which][slot] = self.sum_of(which, place, slot, stage)
+                source = self.staged[which].at[slot]
+            pltpu.make_async_remote_copy(
+                src_ref=source,
+                dst_ref=self.received[which].at[slot],
+                send_sem=self.send_sem.at[which],
+                recv_sem=self.recv_sem.at[which, self.sem_at(which, stage, slot)[0]],
+                device_id=(flip(self.me, order[stage]),),
+                device_id_type=MESH,
+            ).start()
+
+    def finish(self, reduced, squares, own_squares, small_send, small_recv):
+        me, devices = self.me, self.devices
+        own = jnp.zeros((1, LANES), jnp.float32)
+        for which in (2, 1, 0):
+            value = self.sum_of(which, me, 0, self.steps)
+            rows, width = value.shape
+            parts = width // LANES
+            for part in range(parts):
+                piece = value[:, part * LANES : (part + 1) * LANES]
+                reduced[which][pl.ds(part, rows, stride=parts), :] = piece
+                own = own + jnp.sum(piece * piece, axis=0, keepdims=True)
+        own_squares[...] = own
+        squares[0] = own
+
+        @pl.loop(1, devices)
+        def _(shift):
+            pltpu.make_async_remote_copy(
+                src_ref=own_squares,
+                dst_ref=squares.at[shift],
+                send_sem=small_send,
+                recv_sem=small_recv,
+                device_id=((me + shift) % devices,),
+                device_id_type=MESH,
+            ).start()
+
+        for which in range(3):
+            drain(
+                self.received[which], devices - 1, self.send_sem.at[which],
+                self.recv_sem.at[which, 0], flip(me, 1),
+            ).wait_send()
+        small = drain(squares, devices - 1, small_send, small_recv, flip(me, 1))
+        small.wait_send()
+        small.wait_recv()
+
+
 def sum_kernel(devices, *refs):
     grads, reduced, squares = refs[:3], refs[3:6], refs[6]
     received, staged = refs[7:10], refs[10:13]
@@ -525,14 +716,14 @@
         load.start()
     shards, features = held[:3], held[3]
     barrier = pltpu.get_barrier_semaphore()
-    greet(me, devices, barrier)
-    gather = Gather(me, devices, fulls, gather_send, gather_recv)
+    greet_partners(me, devices, barrier)
+    gather = GroupGather(me, devices, fulls, gather_send, gather_recv)
     for load in loads[:3]:
         load.wait()
     gather.fill(shards)
     loads[3].wait()
     normalize(features, normalized)
-    pl.semaphore_wait(barrier, devices - 1)
+    pl.semaphore_wait(barrier, gather.steps)
     gather.pass_on()
     gather.arrive(0)
     project_up(normalized, up_mat, activation, hidden)
@@ -543,7 +734,7 @@
         loss_scale, frame_lens, label_lens, labels, log_probs, emitted, alpha_rows, beta_rows,
         logit_grad,
     )
-    total = Sum(me, devices, grads, received, staged, send_sem, recv_sem)
+    total = GroupSum(me, devices, grads, received, staged, send_sem, recv_sem)
     pending = [list(range(total.steps)) for _ in range(3)]
 
     def advance(*whiches):
@@ -565,7 +756,7 @@
     advance(2)
     while any(pending):
         advance(1, 0, 2)
-    total.finish(devices, reduced, squares, own_squares, small_send, small_recv)
+    total.finish(reduced, squares, own_squares, small_send, small_recv)
     gather.close()
 
 
@@ -586,13 +777,13 @@
         scratch_shapes=[pltpu.VMEM(block, jnp.bfloat16) for block in blocks]
         + wide * 3
         + [
-            pltpu.SemaphoreType.DMA((3, devices)),
-            pltpu.SemaphoreType.DMA((3, devices)),
+            pltpu.SemaphoreType.DMA((3,)),
+            pltpu.SemaphoreType.DMA((3, gather_sems(devices))),
             pltpu.VMEM((1, LANES), jnp.float32),
-            pltpu.SemaphoreType.DMA((3, devices)),
-            pltpu.SemaphoreType.DMA((3, devices)),
-            pltpu.SemaphoreType.DMA((devices,)),
-            pltpu.SemaphoreType.DMA((devices,)),
+            pltpu.SemaphoreType.DMA((3,)),
+            pltpu.SemaphoreType.DMA((3, sum_groups(devices.bit_length() - 1)[1])),
+            pltpu.SemaphoreType.DMA,
+            pltpu.SemaphoreType.DMA,
         ]
         + step_scratch(total, frames)
         + [pltpu.VMEM(array.shape, array.dtype) for array in (*weights, features)]

time: 75.5 us -> 71.6 us (0.948)
  Pallas kernels: 74.6 us -> 70.7 us
    pallas_call x1, Pallas kernels: 72.8 us -> 68.9 us  [fused_step(): pl.pallas_call(functools.partial(fused_kernel, devices, loss_scale), out_...]
where the time goes in v1:
time: 71.6 us; the launch traced here: 71.3 us
  Pallas kernels  70.7 us (99%)
    pallas_call x1, Pallas kernels, fused_step(): pl.pallas_call(functools.partial(fused_kernel, devices, loss_scale), out_...  68.9 us
    pallas_call x1, Pallas kernels, adam(): pl.pallas_call(adam_kernel, out_shape=shapes * 3, in_specs=[VMEM] * 13, o...  1.81 us

profile of v1, /device:TPU:0, one launch (start us, length us, event | category | flops | bytes accessed | tf_op | source)
XLA Modules:
  0.0 71.3 jit_solution(12963407508430845696)
XLA Ops:
  0.6 68.9 %fused_step.1 = (f32[64,128]{1,0:T(8,128)}, f32[64,128]{1,0:T(8,128)}, f32[16,128]{1,0:T(8,128)}, f32[32,1,128]{2,1,0:T(1,128)}) custom-call(s32[2]{0:T(128)} %refs_0_.1, s32[2]{0:T(128)} %refs_1_.1, bf16[512,256]{1,0:T(8,128)(2,1)} %bitcast.19, s32[2,48]{1,0:T(2,128)} %refs_3_.1, f32[64,128]{1,0:T(8,128)} %bitcast.20, f32[64,128]{1,0:T(8,128)} %bitcast.22, ...), custom_call_target="tpu_custom_call" | custom-call | tf_op jit(solution)/shard_map/fused_step/pallas_call | solution.py:771
  69.5 1.8 %adam.1 = (f32[64,128]{1,0:T(8,128)}, f32[64,128]{1,0:T(8,128)}, f32[16,128]{1,0:T(8,128)}, f32[64,128]{1,0:T(8,128)}, f32[64,128]{1,0:T(8,128)}, /*index=5*/f32...) custom-call(f32[32,1,128]{2,1,0:T(1,128)} %get-tuple-element.22.squares, f32[64,128]{1,0:T(8,128)} %bitcast.21, ...), custom_call_target="tpu_custom_call" | custom-call | tf_op jit(solution)/shard_map/adam/pallas_call | solution.py:842

commit v2 on v1

--- a/solution.py
+++ b/solution.py
@@ -16,6 +16,8 @@
 first_correction = 1.0 - (0.9**10) ** 10
 second_correction = 1.0 - (0.999**10) ** 10
 negative = -1e30
+LOG2E = 1.4426950408889634
+PARTS = 2
 VMEM = pl.BlockSpec(memory_space=pltpu.VMEM)
 SMEM = pl.BlockSpec(memory_space=pltpu.SMEM)
 HBM = pl.BlockSpec(memory_space=pltpu.HBM)
@@ -286,10 +288,74 @@
         block_out[rows, :] = out_rows
         logits = dot_rows(out_rows, out_mat[...].reshape(D, VOCAB))
         top = jnp.max(logits, axis=1, keepdims=True)
-        low = logits - top
-        log_probs[rows, :] = low - jnp.log(jnp.sum(jnp.exp(low), axis=1, keepdims=True))
+        low = (logits - top) * LOG2E
+        log_probs[rows, :] = low - jnp.log2(jnp.sum(jnp.exp2(low), axis=1, keepdims=True))
 
     row_blocks(features.shape[0], body)
+
+
+def split_dot(dot, values, picks):
+    high = values.astype(jnp.bfloat16)
+    rest = values - high.astype(jnp.float32)
+    middle = rest.astype(jnp.bfloat16)
+    low = (rest - middle.astype(jnp.float32)).astype(jnp.bfloat16)
+    return dot(high, picks) + (dot(middle, picks) + dot(low, picks))
+
+
+def ctc_rows(frames):
+    return [pltpu.VMEM((frames, 8, LANES), jnp.float32)] * 4 + [
+        pltpu.VMEM((2 * frames, 8, LANES), jnp.float32)
+    ] * 4
+
+
+class Lattice:
+    def __init__(self, parts, sign, skip):
+        self.parts, self.sign = parts, sign
+        self.row = 0 if sign > 0 else 7
+        self.skips = [self.spread(skip, part) > 0.5 for part in range(parts)]
+
+    def spread(self, values, part):
+        if self.sign > 0:
+            return pltpu.roll(values, part, 1, stride=self.parts, stride_axis=0)
+        shift = LANES - part - 7 * self.parts
+        return pltpu.roll(values, shift, 1, stride=self.parts, stride_axis=0)
+
+    def begin(self, blank, label):
+        def whole(values):
+            return jnp.broadcast_to(values[self.row : self.row + 1], (8, LANES))
+
+        blank, label = whole(blank), whole(label)
+        self.blank = [self.spread(blank, part) for part in range(self.parts)]
+        self.label = [self.spread(label, part) for part in range(self.parts + 1)]
+        one = jnp.ones((8, LANES), jnp.float32)
+        self.blank_mass, self.label_mass = [one] * self.parts, [one] * (self.parts + 1)
+
+    def next_rows(self, values):
+        return pltpu.roll(values, 7 if self.sign > 0 else 1, 0)
+
+    def advance(self, emit_blank, emit_label, parts):
+        blank, label, blank_mass, label_mass = [], [], [], []
+        for part in range(parts):
+            b, l, l1 = self.blank[part], self.label[part], self.label[part + 1]
+            bm, lm, lm1 = self.blank_mass[part], self.label_mass[part], self.label_mass[part + 1]
+            top = jnp.maximum(b, l1)
+            mass = bm * jnp.exp2(b - top) + lm1 * jnp.exp2(l1 - top)
+            above = jnp.where(self.skips[part], top, b)
+            above_mass = jnp.where(self.skips[part], mass, bm)
+            peak = jnp.maximum(l, above)
+            peak_mass = lm * jnp.exp2(l - peak) + above_mass * jnp.exp2(above - peak)
+            if part == 0:
+                result = (top, mass, peak, peak_mass)
+            blank.append(top + emit_blank)
+            label.append(peak + self.spread(emit_label, part))
+            blank_mass.append(mass)
+            label_mass.append(peak_mass)
+        if parts == self.parts:
+            label.append(self.next_rows(label[0]))
+            label_mass.append(self.next_rows(label_mass[0]))
+        self.blank, self.label = blank, label
+        self.blank_mass, self.label_mass = blank_mass, label_mass
+        return result
 
 
 def ctc_grad(
@@ -299,19 +365,20 @@
     labels,
     log_probs,
     emitted,
+    emitted_blank,
     alpha_rows,
     beta_rows,
     logit_grad,
 ):
     utterances, label_count = labels.shape
     frames = log_probs.shape[0] // utterances
-    states = 2 * label_count + 1
-
+    half = LANES // utterances
+    depth = 8 * PARTS
+    assert label_count + depth <= half and frames % depth == 0
+
+    lane_row = lax.broadcasted_iota(jnp.int32, (8, LANES), 1)
     label_ids = lax.broadcasted_iota(jnp.int32, (label_count, LANES), 0)
-    state_at = lax.broadcasted_iota(jnp.int32, (label_count, LANES), 1)
-    spread_now = (state_at == 2 * label_ids + 1).astype(jnp.bfloat16)
-    spread_back = (state_at == 2 * label_ids + 3).astype(jnp.bfloat16)
-    spread_ahead = (state_at == 2 * label_ids - 1).astype(jnp.bfloat16)
+    spread_lanes = lax.broadcasted_iota(jnp.int32, (label_count, LANES), 1)
     label_rows = jnp.concatenate(
         [
             labels[...].astype(jnp.float32),
@@ -319,97 +386,114 @@
         ],
         axis=0,
     ).astype(jnp.bfloat16)
-    extended = dot_rows(label_rows, spread_now)
-    earlier = dot_rows(label_rows, spread_back)
-    later = dot_rows(label_rows, spread_ahead)
-    row_ids = lax.broadcasted_iota(jnp.int32, (8, LANES), 0)
-    lane_ids = lax.broadcasted_iota(jnp.int32, (8, LANES), 1)
-    may_skip = (extended > 0.5) & (extended != earlier)
-    skip_later = (later > 0.5) & (later != extended)
-    skip_add = jnp.where(may_skip, 0.0, negative)
-    later_add = jnp.where(skip_later, 0.0, negative)
-    ends = jnp.full((8, LANES), -9, jnp.int32)
-    first_frame = jnp.full((8, LANES), -9, jnp.int32)
+    extended = jnp.zeros((8, LANES), jnp.float32)
     for utterance in range(utterances):
-        ends = jnp.where(row_ids == utterance, 2 * label_lens[utterance], ends)
-        first_frame = jnp.where(row_ids == utterance, frame_lens[utterance] - 1, first_frame)
-    finish = jnp.where((lane_ids == ends) | (lane_ids == ends - 1), 0.0, negative)
-
-    emitted[...] = jnp.full(emitted.shape, negative, jnp.float32)
+        spread = (spread_lanes == label_ids + half * utterance + 1).astype(jnp.bfloat16)
+        placed = dot_rows(label_rows, spread)[utterance : utterance + 1]
+        extended = extended + jnp.broadcast_to(placed, (8, LANES))
+    skip = jnp.where(extended != pltpu.roll(extended, 1, 1), 1.0, 0.0)
+    skip_back = pltpu.roll(skip, LANES - 1, 1)
+
     vocab_ids = lax.broadcasted_iota(jnp.int32, (VOCAB, LANES), 0).astype(jnp.float32)
-    lanes_wide = lax.broadcasted_iota(jnp.int32, (VOCAB, LANES), 1)
+    vocab_lanes = lax.broadcasted_iota(jnp.int32, (VOCAB, LANES), 1)
     frame_lanes = lax.broadcasted_iota(jnp.int32, (frames, LANES), 1)
     onehots = []
+    picked = None
+    blanks = None
     for utterance in range(utterances):
-        onehot = jnp.where(
-            (vocab_ids == extended[utterance : utterance + 1, :]) & (lanes_wide < states), 1.0, 0.0
+        rows = slice(utterance * frames, (utterance + 1) * frames)
+        first = half * utterance + 1
+        mine = (vocab_lanes >= first) & (vocab_lanes < first + label_count)
+        onehot = jnp.where((vocab_ids == extended[0:1, :]) & mine, 1.0, 0.0).astype(jnp.bfloat16)
+        onehots.append(onehot)
+        picks = split_dot(dot_rows, log_probs[rows, :], onehot)
+        blank = jnp.broadcast_to(log_probs[rows, 0:1], (frames, LANES))
+        if utterance == 0:
+            picked, blanks = picks, blank
+        else:
+            picked = jnp.where(frame_lanes < half * utterance, picked, picks)
+            blanks = jnp.where(frame_lanes < half * utterance, blanks, blank)
+    place = frame_lanes % half
+    emitted[...] = jnp.where((place >= 1) & (place <= label_count), picked, negative)
+    emitted_blank[...] = blanks
+
+    forward = Lattice(PARTS, 1, skip)
+    backward = Lattice(PARTS, -1, skip_back)
+    start = jnp.full((8, LANES), negative, jnp.float32)
+    start_back = start
+    for utterance in range(utterances):
+        first = half * utterance + 1
+        start = jnp.where(lane_row == first, 0.0, start)
+        start_back = jnp.where(
+            lane_row == first + label_lens[utterance] - 1, 0.0, start_back
         )
-        onehots.append(onehot)
-        picked = jnp.dot(
-            log_probs[utterance * frames : (utterance + 1) * frames, :],
-            onehot,
-            precision=lax.Precision.HIGHEST,
-            preferred_element_type=jnp.float32,
+    nothing = jnp.full((8, LANES), negative, jnp.float32)
+
+    def row_of(ref, frame):
+        return jnp.broadcast_to(ref[pl.ds(frame, 1), :], (8, LANES))
+
+    def block(at, carry):
+        forward.begin(*carry[:2])
+        backward.begin(*carry[2:])
+        for level in range(depth):
+            frame = at * depth + level
+            needed = min(PARTS, depth - level)
+            result = forward.advance(row_of(emitted_blank, frame), row_of(emitted, frame), needed)
+            for ref, value in zip(alpha_rows, result):
+                ref[frame] = value
+            emit = emit_blank = None
+            for utterance in range(utterances):
+                back = jnp.maximum(frame_lens[utterance] - 1 - frame, 0)
+                mine, mine_blank = row_of(emitted, back), row_of(emitted_blank, back)
+                if utterance == 0:
+                    emit, emit_blank = mine, mine_blank
+                else:
+                    emit = jnp.where(lane_row < half * utterance, emit, mine)
+                    emit_blank = jnp.where(lane_row < half * utterance, emit_blank, mine_blank)
+            result = backward.advance(emit_blank, emit, needed)
+            for ref, value in zip(beta_rows, result):
+                ref[frames - 1 - frame] = value
+        return tuple(
+            values[0] + jnp.log2(mass[0])
+            for lattice in (forward, backward)
+            for values, mass in (
+                (lattice.blank, lattice.blank_mass), (lattice.label, lattice.label_mass)
+            )
         )
-        emitted[:, utterance, :] = jnp.where(frame_lanes < states, picked, negative)
-
-    def log_three(one, two, three):
-        top = jnp.maximum(jnp.maximum(one, two), three)
-        return top + jnp.log(jnp.exp(one - top) + jnp.exp(two - top) + jnp.exp(three - top))
-
-    def ahead(values, count):
-        return pltpu.roll(values, count, 1) if count else values
-
-    def behind(values, count):
-        return pltpu.roll(values, LANES - count, 1) if count else values
-
-    skips = [ahead(skip_add, count) for count in range(3)]
-    later_skips = [behind(later_add, count) for count in range(3)]
-    finishes = [behind(finish, count) for count in range(3)]
-
-    def advance(pair, carry):
-        alpha, weighted = carry
-        frame = 2 * pair
-        back = frames - 1 - frame
-        moved = [ahead(alpha, count) for count in range(5)]
-        other = [behind(weighted, count) for count in range(5)]
-        emit, emit_back = emitted[frame], emitted[back]
-        ends_here = first_frame == back
-        firsts, lasts = [], []
-        for count in range(3):
-            base = log_three(moved[count], moved[count + 1], moved[count + 2] + skips[count])
-            rest = log_three(other[count], other[count + 1], other[count + 2] + later_skips[count])
-            rest = jnp.where(ends_here, finishes[count], rest)
-            if count == 0:
-                alpha_rows[frame] = base
-                beta_rows[back] = rest
-            firsts.append(base + ahead(emit, count))
-            lasts.append(rest + behind(emit_back, count))
-        base = log_three(firsts[0], firsts[1], firsts[2] + skips[0])
-        rest = log_three(lasts[0], lasts[1], lasts[2] + later_skips[0])
-        rest = jnp.where(first_frame == back - 1, finish, rest)
-        alpha_rows[frame + 1] = base
-        beta_rows[back - 1] = rest
-        return (base + emitted[frame + 1], rest + emitted[back - 1])
-
-    nothing = jnp.full((8, LANES), negative, jnp.float32)
-    start = jnp.where(lane_ids == 0, 0.0, negative)
-    lax.fori_loop(0, frames // 2, advance, (start, nothing), unroll=8)
+
+    lax.fori_loop(0, frames // depth, block, (start, nothing, start_back, nothing))
 
     frame_ids = lax.broadcasted_iota(jnp.int32, (frames, LANES), 0)
+    alphas = [ref[:, forward.row, :] for ref in alpha_rows]
+    betas, alive = [], None
+    for ref in beta_rows:
+        value = None
+        for utterance in range(utterances):
+            mine = ref[pl.ds(frames - frame_lens[utterance], frames), backward.row, :]
+            value = mine if value is None else jnp.where(frame_lanes < half * utterance, value, mine)
+        betas.append(value)
+    betas[0], betas[1] = pltpu.roll(betas[0], 1, 1), pltpu.roll(betas[1], 1, 1)
+    joint_blank = alphas[0] + emitted_blank[...] + betas[0]
+    joint_label = alphas[2] + emitted[...] + betas[2]
+    blank_mass, label_mass = alphas[1] * betas[1], alphas[3] * betas[3]
+    both = jnp.maximum(joint_blank, joint_label)
     for utterance in range(utterances):
-        joint = (
-            alpha_rows[:, utterance, :] + emitted[:, utterance, :] + beta_rows[:, utterance, :]
-        )
-        top = jnp.max(joint, axis=1, keepdims=True)
-        mass = jnp.exp(joint - top)
-        share = mass / jnp.sum(mass, axis=1, keepdims=True)
-        occupancy = jnp.where(frame_ids < frame_lens[utterance], share, 0.0)
-        gamma = dot_last(occupancy, onehots[utterance], lax.Precision.HIGHEST)
         rows = slice(utterance * frames, (utterance + 1) * frames)
-        probs = jnp.exp(log_probs[rows, :])
-        held = jnp.sum(occupancy, axis=1, keepdims=True)
-        logit_grad[rows, :] = (loss_scale * (probs * held - gamma)).astype(jnp.bfloat16)
+        first = half * utterance
+        mine = (frame_lanes >= first) & (frame_lanes < first + half)
+        top = jnp.max(jnp.where(mine, both, negative), axis=1, keepdims=True)
+        live = mine & (frame_ids < frame_lens[utterance])
+        label = jnp.where(live, label_mass * jnp.exp2(joint_label - top), 0.0)
+        blank = jnp.where(live, blank_mass * jnp.exp2(joint_blank - top), 0.0)
+        blank_sum = jnp.sum(blank, axis=1, keepdims=True)
+        total = jnp.sum(label, axis=1, keepdims=True) + blank_sum
+        kept = frame_ids[:, 0:1] < frame_lens[utterance]
+        scale = jnp.where(kept, 1.0 / jnp.where(kept, total, 1.0), 0.0)
+        gamma = split_dot(dot_last, label * scale, onehots[utterance])
+        vocab_at = lax.broadcasted_iota(jnp.int32, (frames, VOCAB), 1)
+        gamma = gamma + jnp.where(vocab_at == 0, blank_sum * scale, 0.0)
+        probs = jnp.exp2(log_probs[rows, :]) * jnp.where(kept, 1.0, 0.0)
+        logit_grad[rows, :] = (loss_scale * (probs - gamma)).astype(jnp.bfloat16)
 
 
 def grad_ff(logit_grad, out_mat, ff_grad):
@@ -450,19 +534,19 @@
     hidden,
     block_out,
     log_probs,
-    emitted,
-    alpha_rows,
-    beta_rows,
     logit_grad,
     ff_grad,
     act_grad,
+    emitted,
+    emitted_blank,
+    *lattice_rows,
 ):
     normalize(features, normalized)
     project_up(normalized, up_mat, activation, hidden)
     project_down(features, hidden, down_mat, out_mat, block_out, log_probs)
     ctc_grad(
-        loss_scale, frame_lens, label_lens, labels, log_probs, emitted, alpha_rows, beta_rows,
-        logit_grad,
+        loss_scale, frame_lens, label_lens, labels, log_probs, emitted, emitted_blank,
+        lattice_rows[:4], lattice_rows[4:], logit_grad,
     )
     grad_ff(logit_grad, out_mat, ff_grad)
     grad_act(ff_grad, down_mat, activation, act_grad)
@@ -478,13 +562,12 @@
         pltpu.VMEM((total, FF), jnp.bfloat16),
         pltpu.VMEM((total, D), jnp.bfloat16),
         pltpu.VMEM((total, VOCAB), jnp.float32),
-        pltpu.VMEM((frames, 8, LANES), jnp.float32),
-        pltpu.VMEM((frames, 8, LANES), jnp.float32),
-        pltpu.VMEM((frames, 8, LANES), jnp.float32),
         pltpu.VMEM((total, VOCAB), jnp.bfloat16),
         pltpu.VMEM((total, D), jnp.bfloat16),
         pltpu.VMEM((total, FF), jnp.bfloat16),
-    ]
+        pltpu.VMEM((frames, LANES), jnp.float32),
+        pltpu.VMEM((frames, LANES), jnp.float32),
+    ] + ctc_rows(frames)
 
 
 def local_step(loss_scale, frame_lens, label_lens, features, labels, up_mat, down_mat, out_mat):
@@ -704,8 +787,9 @@
     fulls, grads, received, staged = refs[11:14], refs[14:17], refs[17:20], refs[20:23]
     gather_send, gather_recv, own_squares, send_sem, recv_sem, small_send, small_recv = refs[23:30]
     normalized, activation, hidden, block_out, log_probs = refs[30:35]
-    emitted, alpha_rows, beta_rows, logit_grad, ff_grad, act_grad = refs[35:41]
-    held, load_sem = refs[41:45], refs[45]
+    logit_grad, ff_grad, act_grad, emitted, emitted_blank = refs[35:40]
+    alpha_rows, beta_rows = refs[40:44], refs[44:48]
+    held, load_sem = refs[48:52], refs[52]
     up_mat, down_mat, out_mat = fulls
     me = lax.axis_index("dp")
     loads = [
@@ -731,8 +815,8 @@
     gather.arrive(2)
     project_down(features, hidden, down_mat, out_mat, block_out, log_probs)
     ctc_grad(
-        loss_scale, frame_lens, label_lens, labels, log_probs, emitted, alpha_rows, beta_rows,
-        logit_grad,
+        loss_scale, frame_lens, label_lens, labels, log_probs, emitted, emitted_blank, alpha_rows,
+        beta_rows, logit_grad,
     )
     total = GroupSum(me, devices, grads, received, staged, send_sem, recv_sem)
     pending = [list(range(total.steps)) for _ in range(3)]

time: 71.6 us -> 60.8 us (0.85)
  Pallas kernels: 70.7 us -> 59.9 us
    pallas_call x1, Pallas kernels: 68.9 us -> 58.1 us  [fused_step(): pl.pallas_call(functools.partial(fused_kernel, devices, loss_scale), out_...]
where the time goes in v2:
time: 60.8 us; the launch traced here: 60.5 us
  Pallas kernels  59.9 us (99%)
  between operations  0.65 us (1%)
    pallas_call x1, Pallas kernels, fused_step(): pl.pallas_call(functools.partial(fused_kernel, devices, loss_scale), out_...  58.1 us
    pallas_call x1, Pallas kernels, adam(): pl.pallas_call(adam_kernel, out_shape=shapes * 3, in_specs=[VMEM] * 13, o...  1.81 us

profile of v2, /device:TPU:0, one launch (start us, length us, event | category | flops | bytes accessed | tf_op | source)
XLA Modules:
  0.0 60.5 jit_solution(10182596878300881765)
XLA Ops:
  0.6 58.1 %fused_step.1 = (f32[64,128]{1,0:T(8,128)}, f32[64,128]{1,0:T(8,128)}, f32[16,128]{1,0:T(8,128)}, f32[32,1,128]{2,1,0:T(1,128)}) custom-call(s32[2]{0:T(128)} %refs_0_.1, s32[2]{0:T(128)} %refs_1_.1, bf16[512,256]{1,0:T(8,128)(2,1)} %bitcast.19, s32[2,48]{1,0:T(2,128)} %refs_3_.1, f32[64,128]{1,0:T(8,128)} %bitcast.20, f32[64,128]{1,0:T(8,128)} %bitcast.22, ...), custom_call_target="tpu_custom_call" | custom-call | tf_op jit(solution)/shard_map/fused_step/pallas_call | solution.py:855
  58.7 1.8 %adam.1 = (f32[64,128]{1,0:T(8,128)}, f32[64,128]{1,0:T(8,128)}, f32[16,128]{1,0:T(8,128)}, f32[64,128]{1,0:T(8,128)}, f32[64,128]{1,0:T(8,128)}, /*index=5*/f32...) custom-call(f32[32,1,128]{2,1,0:T(1,128)} %get-tuple-element.22.squares, f32[64,128]{1,0:T(8,128)} %bitcast.21, ...), custom_call_target="tpu_custom_call" | custom-call | tf_op jit(solution)/shard_map/adam/pallas_call | solution.py:926

commit v3 on v2

--- a/solution.py
+++ b/solution.py
@@ -118,12 +118,19 @@
     )
 
 
-class GroupGather:
-    def __init__(self, me, devices, fulls, send_sem, recv_sem):
-        self.me, self.devices, self.fulls = me, devices, fulls
+def flat(stages):
+    return [bit for stage in stages for bit in stage]
+
+
+def move(me, offset, bits):
+    return place_with(me, bits, offset)
+
+
+class StagedGather:
+    def __init__(self, me, plans, fulls, send_sem, recv_sem):
+        self.me, self.plans, self.fulls = me, plans, fulls
         self.send_sem, self.recv_sem = send_sem, recv_sem
-        self.orders = bit_orders(devices)
-        self.steps = len(self.orders[0])
+        self.units = [gather_units(plan) for plan in plans]
 
     def fill(self, shards):
         for shard, full in zip(shards, self.fulls):
@@ -134,21 +141,22 @@
                     pl.ds(part, rows, stride=parts), :
                 ].astype(jnp.bfloat16)
 
-    def sem_at(self, stage, group):
-        return stage * (stage + 1) // 2 + (group if stage < self.steps - 1 else 0)
-
-    def send(self, which, patterns, stage, group):
-        order, full = self.orders[which], self.fulls[which]
-        for pattern in patterns:
-            owner = place_with(self.me, order[:stage], pattern)
-            pltpu.make_async_remote_copy(
-                src_ref=full.at[owner],
-                dst_ref=full.at[owner],
-                send_sem=self.send_sem.at[which],
-                recv_sem=self.recv_sem.at[which, self.sem_at(stage, group)],
-                device_id=(flip(self.me, order[stage]),),
-                device_id_type=MESH,
-            ).start()
+    def send(self, which, source, first):
+        plan, full = self.plans[which], self.fulls[which]
+        for stage in range(first, len(plan)):
+            for offset in subsets(plan[stage])[1:][::-1]:
+                sem = self.units[which][1][stage, offset, source]
+                peer = move(self.me, offset, plan[stage])
+                for pattern in self.units[which][0][source][0] if source else [0]:
+                    owner = move(self.me, pattern, flat(plan[:stage]))
+                    pltpu.make_async_remote_copy(
+                        src_ref=full.at[owner],
+                        dst_ref=full.at[owner],
+                        send_sem=self.send_sem.at[which],
+                        recv_sem=self.recv_sem.at[which, sem],
+                        device_id=(peer,),
+                        device_id_type=MESH,
+                    ).start()
 
     def drain(self, which, blocks, at):
         return drain(
@@ -158,39 +166,49 @@
 
     def pass_on(self):
         for which in range(3):
-            for stage in range(self.steps):
-                self.send(which, [0], stage, 0)
-        for stage in range(self.steps - 1):
-            for group in range(stage + 1):
-                for which in range(3):
-                    order = self.orders[which]
-                    patterns = [0]
-                    if group:
-                        patterns = [at + order[group - 1] for at in subsets(order[: group - 1])]
-                    self.drain(which, len(patterns), self.sem_at(stage, group)).wait_recv()
-                    patterns = [pattern + order[stage] for pattern in patterns]
-                    for later in range(stage + 1, self.steps):
-                        self.send(which, patterns, later, stage + 1)
+            self.send(which, None, 0)
+        names = [list(units[0]) for units in self.units]
+        for at in range(max(len(some) for some in names)):
+            for which in range(3):
+                if at < len(names[which]):
+                    name = names[which][at]
+                    patterns, sem = self.units[which][0][name]
+                    self.drain(which, len(patterns), sem).wait_recv()
+                    self.send(which, name, name[0] + 1)
 
     def arrive(self, which):
-        last = self.steps - 1
-        self.drain(which, 1 << last, self.sem_at(last, 0)).wait_recv()
+        before = 1 << len(flat(self.plans[which][:-1]))
+        self.drain(which, before, self.units[which][2] - 1).wait_recv()
 
     def close(self):
         for which in range(3):
-            self.drain(which, self.devices - 1, 0).wait_send()
-
-
-def gather_sems(devices):
-    steps = devices.bit_length() - 1
-    return (steps - 1) * steps // 2 + 1
-
-
-def greet_partners(me, devices, barrier):
-    for step in range(devices.bit_length() - 1):
-        pl.semaphore_signal(
-            barrier, inc=1, device_id=(flip(me, 1 << step),), device_id_type=MESH
-        )
+            before = 1 << len(flat(self.plans[which]))
+            self.drain(which, before - 1, 0).wait_send()
+
+
+def gather_units(plan):
+    units, sems, count = {}, {}, 0
+    for stage, bits in enumerate(plan):
+        sources = {None: [0], **{name: patterns for name, (patterns, _) in units.items()}}
+        for name, patterns in sources.items():
+            for offset in subsets(bits)[1:]:
+                sems[stage, offset, name] = count
+                if stage < len(plan) - 1:
+                    units[stage, offset, name] = ([offset + at for at in patterns], count)
+                    count += 1
+    return units, sems, count + 1
+
+
+def greet_stages(me, plan, barrier):
+    for bits in plan:
+        for offset in subsets(bits)[1:]:
+            pl.semaphore_signal(
+                barrier, inc=1, device_id=(move(me, offset, bits),), device_id_type=MESH
+            )
+
+
+def stage_partners(plan):
+    return sum((1 << len(bits)) - 1 for bits in plan)
 
 
 def greet(me, devices, barrier):
@@ -661,81 +679,94 @@
             small_copy(shift).wait()
 
 
-def chunks(blocks):
-    if blocks >= 4:
-        return [blocks // 4, blocks // 4, blocks // 2]
-    return [1] * blocks
-
-
-def sum_groups(steps):
-    groups, sems = [], 0
-    for stage in range(steps):
-        sizes = chunks(1 << (steps - 1 - stage))
-        groups.append((sems, sizes))
-        sems += len(sizes)
-    return groups, sems
-
-
-class GroupSum:
-    def __init__(self, me, devices, grads, received, staged, send_sem, recv_sem):
-        self.me, self.devices = me, devices
+def sum_pieces(plan):
+    pieces = {}
+    for stage, bits in enumerate(plan):
+        for offset in subsets(bits)[1:]:
+            for after in subsets(plan[stage + 1]) if stage + 1 < len(plan) else [0]:
+                pieces[stage, offset, after] = len(pieces)
+    return pieces
+
+
+class StagedSum:
+    def __init__(self, me, plans, narrow, grads, received, staged, send_sem, recv_sem):
+        self.me, self.plans, self.narrow = me, plans, narrow
         self.grads, self.received, self.staged = grads, received, staged
         self.send_sem, self.recv_sem = send_sem, recv_sem
-        self.orders = [order[::-1] for order in bit_orders(devices)]
-        self.steps = len(self.orders[0])
-        self.groups, _ = sum_groups(self.steps)
+        self.pieces = [sum_pieces(plan) for plan in plans]
         self.seen = set()
 
-    def slots(self, which, stage):
-        order = self.orders[which]
-        return [
-            offset + order[stage] for offset in subsets(order[stage + 1 :][::-1])[::-1]
-        ]
-
-    def sem_at(self, which, stage, slot):
-        at = self.slots(which, stage).index(slot)
-        sem, sizes = self.groups[stage]
-        for size in sizes:
-            if at < size:
-                return sem, size
-            at, sem = at - size, sem + 1
-
-    def sum_of(self, which, place, pattern, stage):
-        value = self.grads[which][place]
-        for at, bit in enumerate(self.orders[which][:stage]):
-            sem, size = self.sem_at(which, at, pattern + bit)
-            if (which, sem) not in self.seen:
-                self.seen.add((which, sem))
-                drain(
-                    self.received[which], size, self.send_sem.at[which],
-                    self.recv_sem.at[which, sem], flip(self.me, bit),
-                ).wait_recv()
-            value = value + self.received[which][pattern + bit]
+    def index(self, which, pattern):
+        bits = flat(self.plans[which])
+        return sum(1 << at for at, bit in enumerate(bits[::-1]) if pattern & bit)
+
+    def wide(self, which, stage):
+        return 3 * (stage in self.narrow[which]) + which
+
+    def put(self, which, value):
+        bits = flat(self.plans[which])[::-1]
+        blocks, rows, width = self.grads[which].shape
+        own = [(self.me // bit) % 2 for bit in bits]
+        for block in range(blocks):
+            slot = 0
+            for at, bit in enumerate(bits):
+                slot = slot + (1 << at) * (1 - own[at] if block & bit else own[at])
+            self.grads[which][slot] = value[block * rows : (block + 1) * rows, :]
+
+    def piece(self, which, stage, pattern):
+        plan = self.plans[which]
+        offset = sum(bit for bit in plan[stage] if pattern & bit)
+        after = 0
+        if stage + 1 < len(plan):
+            after = sum(bit for bit in plan[stage + 1] if pattern & bit)
+        return stage, offset, after
+
+    def copy(self, which, name):
+        stage, offset, after = name
+        start = self.index(which, offset + after)
+        blocks = pl.ds(start, 1 << len(flat(self.plans[which][stage + 2 :])))
+        at = self.wide(which, stage)
+        source = self.grads[which] if stage == 0 else self.staged[at]
+        return pltpu.make_async_remote_copy(
+            src_ref=source.at[blocks],
+            dst_ref=self.received[at].at[blocks],
+            send_sem=self.send_sem.at[at],
+            recv_sem=self.recv_sem.at[which, self.pieces[which][name]],
+            device_id=(move(self.me, offset, self.plans[which][stage]),),
+            device_id_type=MESH,
+        )
+
+    def sum_of(self, which, pattern, stage):
+        value = self.grads[which][self.index(which, pattern)]
+        for earlier in range(stage):
+            for offset in subsets(self.plans[which][earlier])[1:]:
+                name = self.piece(which, earlier, pattern + offset)
+                if (which, name) not in self.seen:
+                    self.seen.add((which, name))
+                    self.copy(which, name).wait_recv()
+                slot = self.index(which, pattern + offset)
+                value = value + self.received[self.wide(which, earlier)][slot].astype(jnp.float32)
         return value
 
     def send(self, which, stage):
-        order = self.orders[which]
-        for slot in self.slots(which, stage):
-            place = place_with(self.me, order, slot)
-            if stage == 0:
-                source = self.grads[which].at[place]
-            else:
-                self.staged[which][slot] = self.sum_of(which, place, slot, stage)
-                source = self.staged[which].at[slot]
-            pltpu.make_async_remote_copy(
-                src_ref=source,
-                dst_ref=self.received[which].at[slot],
-                send_sem=self.send_sem.at[which],
-                recv_sem=self.recv_sem.at[which, self.sem_at(which, stage, slot)[0]],
-                device_id=(flip(self.me, order[stage]),),
-                device_id_type=MESH,
-            ).start()
-
-    def finish(self, reduced, squares, own_squares, small_send, small_recv):
-        me, devices = self.me, self.devices
+        plan = self.plans[which]
+        afters = subsets(plan[stage + 1])[::-1] if stage + 1 < len(plan) else [0]
+        for after in afters:
+            for offset in subsets(plan[stage])[1:][::-1]:
+                if stage:
+                    staged = self.staged[self.wide(which, stage)]
+                    for later in subsets(flat(plan[stage + 2 :])):
+                        pattern = offset + after + later
+                        staged[self.index(which, pattern)] = self.sum_of(
+                            which, pattern, stage
+                        ).astype(staged.dtype)
+                self.copy(which, (stage, offset, after)).start()
+
+    def finish(self, devices, reduced, squares, own_squares, small_send, small_recv):
+        me = self.me
         own = jnp.zeros((1, LANES), jnp.float32)
         for which in (2, 1, 0):
-            value = self.sum_of(which, me, 0, self.steps)
+            value = self.sum_of(which, 0, len(self.plans[which]))
             rows, width = value.shape
             parts = width // LANES
             for part in range(parts):
@@ -756,11 +787,17 @@
                 device_id_type=MESH,
             ).start()
 
-        for which in range(3):
-            drain(
-                self.received[which], devices - 1, self.send_sem.at[which],
-                self.recv_sem.at[which, 0], flip(me, 1),
-            ).wait_send()
+        for which, plan in enumerate(self.plans):
+            sent = {}
+            for stage, bits in enumerate(plan):
+                blocks = ((1 << len(bits)) - 1) << len(flat(plan[stage + 1 :]))
+                at = self.wide(which, stage)
+                sent[at] = sent.get(at, 0) + blocks
+            for at, blocks in sent.items():
+                drain(
+                    self.received[at], blocks, self.send_sem.at[at], self.recv_sem.at[which, 0],
+                    flip(me, 1),
+                ).wait_send()
         small = drain(squares, devices - 1, small_send, small_recv, flip(me, 1))
         small.wait_send()
         small.wait_recv()
@@ -781,15 +818,30 @@
     total.finish(devices, reduced, squares, own_squares, small_send, small_recv)
 
 
+def exchange_plans(devices):
+    bits = [1 << k for k in range(devices.bit_length() - 1)]
+    core, near, far = bits[:1], bits[1:3], bits[3:]
+    gathers = ([far, near, core], [far, near, core], [near, far, core])
+    sums = ([core, near, far], [core, near, far], [core, far, near])
+    narrow = ((1, 2), (1,), (1,))
+    return gathers, sums, narrow
+
+
+def meet_plan(devices):
+    bits = [1 << k for k in range(devices.bit_length() - 1)]
+    core, near, far = bits[:1], bits[1:3], bits[3:]
+    return [core, near, far]
+
+
 def fused_kernel(devices, loss_scale, *refs):
     frame_lens, label_lens, features, labels = refs[:4]
     shards, reduced, squares = refs[4:7], refs[7:10], refs[10]
-    fulls, grads, received, staged = refs[11:14], refs[14:17], refs[17:20], refs[20:23]
-    gather_send, gather_recv, own_squares, send_sem, recv_sem, small_send, small_recv = refs[23:30]
-    normalized, activation, hidden, block_out, log_probs = refs[30:35]
-    logit_grad, ff_grad, act_grad, emitted, emitted_blank = refs[35:40]
-    alpha_rows, beta_rows = refs[40:44], refs[44:48]
-    held, load_sem = refs[48:52], refs[52]
+    fulls, grads, received, staged = refs[11:14], refs[14:17], refs[17:23], refs[23:29]
+    gather_send, gather_recv, own_squares, send_sem, recv_sem, small_send, small_recv = refs[29:36]
+    normalized, activation, hidden, block_out, log_probs = refs[36:41]
+    logit_grad, ff_grad, act_grad, emitted, emitted_blank = refs[41:46]
+    alpha_rows, beta_rows = refs[46:50], refs[50:54]
+    held, load_sem = refs[54:58], refs[58]
     up_mat, down_mat, out_mat = fulls
     me = lax.axis_index("dp")
     loads = [
@@ -800,14 +852,15 @@
         load.start()
     shards, features = held[:3], held[3]
     barrier = pltpu.get_barrier_semaphore()
-    greet_partners(me, devices, barrier)
-    gather = GroupGather(me, devices, fulls, gather_send, gather_recv)
+    gathers, sums, narrow = exchange_plans(devices)
+    greet_stages(me, meet_plan(devices), barrier)
+    gather = StagedGather(me, gathers, fulls, gather_send, gather_recv)
     for load in loads[:3]:
         load.wait()
     gather.fill(shards)
     loads[3].wait()
     normalize(features, normalized)
-    pl.semaphore_wait(barrier, gather.steps)
+    pl.semaphore_wait(barrier, stage_partners(meet_plan(devices)))
     gather.pass_on()
     gather.arrive(0)
     project_up(normalized, up_mat, activation, hidden)
@@ -818,29 +871,26 @@
         loss_scale, frame_lens, label_lens, labels, log_probs, emitted, emitted_blank, alpha_rows,
         beta_rows, logit_grad,
     )
-    total = GroupSum(me, devices, grads, received, staged, send_sem, recv_sem)
-    pending = [list(range(total.steps)) for _ in range(3)]
+    total = StagedSum(me, sums, narrow, grads, received, staged, send_sem, recv_sem)
+    pending = [list(range(len(plan))) for plan in sums]
 
     def advance(*whiches):
         for which in whiches:
             if pending[which]:
                 total.send(which, pending[which].pop(0))
 
-    def put(which, value):
-        grads[which][...] = value.reshape(grads[which].shape)
-
     grad_ff(logit_grad, out_mat, ff_grad)
-    put(1, dot_first(hidden[...], ff_grad[...]))
+    total.put(1, dot_first(hidden[...], ff_grad[...]))
     advance(1)
     grad_act(ff_grad, down_mat, activation, act_grad)
     advance(1)
-    put(0, dot_first(normalized[...], act_grad[...]))
+    total.put(0, dot_first(normalized[...], act_grad[...]))
     advance(0)
-    put(2, dot_first(block_out[...], logit_grad[...]))
+    total.put(2, dot_first(block_out[...], logit_grad[...]))
     advance(2)
     while any(pending):
         advance(1, 0, 2)
-    total.finish(reduced, squares, own_squares, small_send, small_recv)
+    total.finish(devices, reduced, squares, own_squares, small_send, small_recv)
     gather.close()
 
 
@@ -851,7 +901,9 @@
         (devices, weight.size // width, width)
         for weight, width in zip(weights, (FF, D, VOCAB))
     ]
+    gathers, sums, _ = exchange_plans(devices)
     wide = [pltpu.VMEM(block, jnp.float32) for block in blocks]
+    both = wide + [pltpu.VMEM(block, jnp.bfloat16) for block in blocks]
     return pl.pallas_call(
         functools.partial(fused_kernel, devices, loss_scale),
         out_shape=[jax.ShapeDtypeStruct(weight.shape, jnp.float32) for weight in weights]
@@ -859,13 +911,14 @@
         in_specs=[SMEM, SMEM, HBM, VMEM] + [HBM] * 3,
         out_specs=[VMEM] * 4,
         scratch_shapes=[pltpu.VMEM(block, jnp.bfloat16) for block in blocks]
-        + wide * 3
+        + wide
+        + both * 2
         + [
             pltpu.SemaphoreType.DMA((3,)),
-            pltpu.SemaphoreType.DMA((3, gather_sems(devices))),
+            pltpu.SemaphoreType.DMA((3, max(gather_units(plan)[2] for plan in gathers))),
             pltpu.VMEM((1, LANES), jnp.float32),
-            pltpu.SemaphoreType.DMA((3,)),
-            pltpu.SemaphoreType.DMA((3, sum_groups(devices.bit_length() - 1)[1])),
+            pltpu.SemaphoreType.DMA((6,)),
+            pltpu.SemaphoreType.DMA((3, max(len(sum_pieces(plan)) for plan in sums))),
             pltpu.SemaphoreType.DMA,
             pltpu.SemaphoreType.DMA,
         ]
@@ -873,10 +926,10 @@
         + [pltpu.VMEM(array.shape, array.dtype) for array in (*weights, features)]
         + [pltpu.SemaphoreType.DMA((4,))],
         compiler_params=pltpu.CompilerParams(
-            collective_id=2, has_side_effects=True, vmem_limit_bytes=67043328
+            collective_id=2, has_side_effects=True, vmem_limit_bytes=34 << 20
         ),
         name="fused_step",
-    )(frame_lens, label_lens, features, labels, *weights)
+    )(*(pltpu.with_memory_space_constraint(array, pltpu.HBM) for array in (frame_lens, label_lens, features, labels, *weights)))
 
 
 def sum_gradients(devices, grads):
@@ -928,7 +981,7 @@
         out_shape=shapes * 3,
         in_specs=[VMEM] * 13,
         out_specs=[VMEM] * 9,
-        compiler_params=pltpu.CompilerParams(vmem_limit_bytes=67043328),
+        compiler_params=pltpu.CompilerParams(vmem_limit_bytes=4 << 20),
         name="adam",
     )(squares, *weights, *firsts, *seconds, *grads)
 

time: 60.8 us -> 48.4 us (0.80)
  Pallas kernels: 59.9 us -> 47.2 us
    pallas_call x1, Pallas kernels: 58.1 us -> 46.3 us  [fused_step(): pl.pallas_call(functools.partial(fused_kernel, devices, loss_scale), out_...]
    pallas_call x1, Pallas kernels: 1.81 us -> 0.87 us  [adam(): pl.pallas_call(adam_kernel, out_shape=shapes * 3, in_specs=[VMEM] * 13, o...]
where the time goes in v3:
time: 48.4 us; the launch traced here: 48 us
  Pallas kernels  47.2 us (98%)
  between operations  0.8 us (2%)
    pallas_call x1, Pallas kernels, fused_step(): pl.pallas_call(functools.partial(fused_kernel, devices, loss_scale), out_...  46.3 us

profile of v3, /device:TPU:0, one launch (start us, length us, event | category | flops | bytes accessed | tf_op | source)
XLA Modules:
  0.0 48.0 jit_solution(11045674230783719185)
XLA Ops:
  0.6 0.0 copy-start
  0.7 0.0 copy-start.1
  0.7 0.0 copy-start.2
  0.7 0.0 copy-start.3
  0.7 0.0 copy-start.4
  0.7 0.0 copy-start.5
  0.7 0.0 copy-start.6
  0.7 0.0 copy-start.7
  0.7 0.0 copy-start.8
  0.7 46.3 %fused_step.1 = (f32[64,128]{1,0:T(8,128)S(1)}, f32[64,128]{1,0:T(8,128)S(1)}, f32[16,128]{1,0:T(8,128)S(1)}, f32[32,1,128]{2,1,0:T(1,128)S(1)}) custom-call(s32[2]{0:T(128)} %refs_0_.1, s32[2]{0:T(128)} %refs_1_.1, bf16[512,256]{1,0:T(8,128)(2,1)} %bitcast.31, s32[2,48]{1,0:T(2,128)} %refs_3_.1, f32[64,128]{1,0:T(8,128)} %bitcast.19, f32[64,128]{1,0:T(8,128)} %bitcast.21, ...), custom_call_target="tpu_custom_call" | custom-call | tf_op jit(solution)/shard_map/fused_step/pallas_call | solution.py:907
  47.1 0.0 copy-done
  47.1 0.0 copy-done.1
  47.1 0.0 copy-done.2
  47.1 0.0 copy-done.3
  47.1 0.0 copy-done.4
  47.1 0.0 copy-done.5
  47.1 0.0 copy-done.6
  47.1 0.0 copy-done.7
  47.2 0.0 copy-done.8
  47.2 0.9 %adam.1 = (f32[64,128]{1,0:T(8,128)}, f32[64,128]{1,0:T(8,128)}, f32[16,128]{1,0:T(8,128)}, f32[64,128]{1,0:T(8,128)}, f32[64,128]{1,0:T(8,128)}, /*index=5*/f32...) custom-call(f32[32,1,128]{2,1,0:T(1,128)S(1)} %get-tuple-element.22.squares, ...), custom_call_target="tpu_custom_call" | custom-call | tf_op jit(solution)/shard_map/adam/pallas_call | solution.py:979
Async XLA Ops:
  0.6 46.4 %copy-start = (f32[8192]{0:T(1024)S(1)}, f32[8192]{0:T(1024)}, u32[]{:S(2)}) copy-start(f32[8192]{0:T(1024)} %param.17) | copy-start | bytes 98308
  0.7 46.4 %copy-start.1 = (f32[8192]{0:T(1024)S(1)}, f32[8192]{0:T(1024)}, u32[]{:S(2)}) copy-start(f32[8192]{0:T(1024)} %param.18) | copy-start | bytes 98308
  0.7 46.4 %copy-start.2 = (f32[8192]{0:T(1024)S(1)}, f32[8192]{0:T(1024)}, u32[]{:S(2)}) copy-start(f32[8192]{0:T(1024)} %param.20) | copy-start | bytes 98308
  0.7 46.4 %copy-start.3 = (f32[8192]{0:T(1024)S(1)}, f32[8192]{0:T(1024)}, u32[]{:S(2)}) copy-start(f32[8192]{0:T(1024)} %param.21) | copy-start | bytes 98308
  0.7 46.4 %copy-start.4 = (f32[8192]{0:T(1024)S(1)}, f32[8192]{0:T(1024)}, u32[]{:S(2)}) copy-start(f32[8192]{0:T(1024)} %param.23) | copy-start | bytes 98308
  0.7 46.4 %copy-start.5 = (f32[8192]{0:T(1024)S(1)}, f32[8192]{0:T(1024)}, u32[]{:S(2)}) copy-start(f32[8192]{0:T(1024)} %param.24) | copy-start | bytes 98308
  0.7 46.4 %copy-start.6 = (f32[2048]{0:T(1024)S(1)}, f32[2048]{0:T(1024)}, u32[]{:S(2)}) copy-start(f32[2048]{0:T(1024)} %param.19) | copy-start | bytes 24580
  0.7 46.4 %copy-start.7 = (f32[2048]{0:T(1024)S(1)}, f32[2048]{0:T(1024)}, u32[]{:S(2)}) copy-start(f32[2048]{0:T(1024)} %param.22) | copy-start | bytes 24580
  0.7 46.4 %copy-start.8 = (f32[2048]{0:T(1024)S(1)}, f32[2048]{0:T(1024)}, u32[]{:S(2)}) copy-start(f32[2048]{0:T(1024)} %param.25) | copy-start | bytes 24580

commit v4 on v3

--- a/solution.py
+++ b/solution.py
@@ -143,17 +143,17 @@
 
     def send(self, which, source, first):
         plan, full = self.plans[which], self.fulls[which]
+        units, sems, _ = self.units[which]
         for stage in range(first, len(plan)):
             for offset in subsets(plan[stage])[1:][::-1]:
-                sem = self.units[which][1][stage, offset, source]
                 peer = move(self.me, offset, plan[stage])
-                for pattern in self.units[which][0][source][0] if source else [0]:
+                for pattern in units[source][0] if source else [0]:
                     owner = move(self.me, pattern, flat(plan[:stage]))
                     pltpu.make_async_remote_copy(
                         src_ref=full.at[owner],
                         dst_ref=full.at[owner],
                         send_sem=self.send_sem.at[which],
-                        recv_sem=self.recv_sem.at[which, sem],
+                        recv_sem=self.recv_sem.at[which, sems[stage, offset, source]],
                         device_id=(peer,),
                         device_id_type=MESH,
                     ).start()
@@ -188,13 +188,18 @@
 
 def gather_units(plan):
     units, sems, count = {}, {}, 0
+    last = len(plan) - 1
     for stage, bits in enumerate(plan):
+        offsets = subsets(bits)[1:]
+        groups = [[offset] for offset in offsets] if stage + 1 < last else [offsets]
         sources = {None: [0], **{name: patterns for name, (patterns, _) in units.items()}}
         for name, patterns in sources.items():
-            for offset in subsets(bits)[1:]:
-                sems[stage, offset, name] = count
-                if stage < len(plan) - 1:
-                    units[stage, offset, name] = ([offset + at for at in patterns], count)
+            for group in groups:
+                for offset in group:
+                    sems[stage, offset, name] = count
+                if stage < last:
+                    arriving = [offset + at for offset in group for at in patterns]
+                    units[stage, tuple(group), name] = (arriving, count)
                     count += 1
     return units, sems, count + 1
 
@@ -270,11 +275,9 @@
 
 
 def row_blocks(total, body):
-    block = min(128, total)
-
-    @pl.loop(0, total // block)
-    def _(step):
-        body(pl.ds(pl.multiple_of(step * block, block), block))
+    block = min(256, total)
+    for step in range(total // block):
+        body(pl.ds(step * block, block))
 
 
 def normalize(features, normalized):
@@ -288,11 +291,12 @@
     row_blocks(features.shape[0], body)
 
 
-def project_up(normalized, up_mat, activation, hidden):
+def project_up(normalized, up_mat, slopes, hidden):
     def body(rows):
         act = dot_rows(normalized[rows, :], up_mat[...].reshape(D, FF))
-        activation[rows, :] = act
-        hidden[rows, :] = (act * (1.0 / (1.0 + jnp.exp(-act)))).astype(jnp.bfloat16)
+        sigmoid = 1.0 / (1.0 + jnp.exp(-act))
+        slopes[rows, :] = sigmoid * (1.0 + act * (1.0 - sigmoid))
+        hidden[rows, :] = (act * sigmoid).astype(jnp.bfloat16)
 
     row_blocks(normalized.shape[0], body)
 
@@ -523,13 +527,10 @@
     row_blocks(logit_grad.shape[0], body)
 
 
-def grad_act(ff_grad, down_mat, activation, act_grad):
+def grad_act(ff_grad, down_mat, slopes, act_grad):
     def body(rows):
-        act = activation[rows, :]
-        sigmoid = 1.0 / (1.0 + jnp.exp(-act))
-        slope = sigmoid * (1.0 + act * (1.0 - sigmoid))
         act_grad[rows, :] = (
-            dot_last(ff_grad[rows, :], down_mat[...].reshape(FF, D)) * slope
+            dot_last(ff_grad[rows, :], down_mat[...].reshape(FF, D)) * slopes[rows, :]
         ).astype(jnp.bfloat16)
 
     row_blocks(ff_grad.shape[0], body)
@@ -548,7 +549,7 @@
     grad_down,
     grad_out,
     normalized,
-    activation,
+    slopes,
     hidden,
     block_out,
     log_probs,
@@ -560,14 +561,14 @@
     *lattice_rows,
 ):
     normalize(features, normalized)
-    project_up(normalized, up_mat, activation, hidden)
+    project_up(normalized, up_mat, slopes, hidden)
     project_down(features, hidden, down_mat, out_mat, block_out, log_probs)
     ctc_grad(
         loss_scale, frame_lens, label_lens, labels, log_probs, emitted, emitted_blank,
         lattice_rows[:4], lattice_rows[4:], logit_grad,
     )
     grad_ff(logit_grad, out_mat, ff_grad)
-    grad_act(ff_grad, down_mat, activation, act_grad)
+    grad_act(ff_grad, down_mat, slopes, act_grad)
     grad_up[...] = dot_first(normalized[...], act_grad[...])
     grad_down[...] = dot_first(hidden[...], ff_grad[...])
     grad_out[...] = dot_first(block_out[...], logit_grad[...])
@@ -681,10 +682,9 @@
 
 def sum_pieces(plan):
     pieces = {}
-    for stage, bits in enumerate(plan):
-        for offset in subsets(bits)[1:]:
-            for after in subsets(plan[stage + 1]) if stage + 1 < len(plan) else [0]:
-                pieces[stage, offset, after] = len(pieces)
+    for stage in range(len(plan)):
+        for after in subsets(plan[stage + 1]) if stage + 1 < len(plan) else [0]:
+            pieces[stage, after] = len(pieces)
     return pieces
 
 
@@ -712,14 +712,6 @@
             for at, bit in enumerate(bits):
                 slot = slot + (1 << at) * (1 - own[at] if block & bit else own[at])
             self.grads[which][slot] = value[block * rows : (block + 1) * rows, :]
-
-    def piece(self, which, stage, pattern):
-        plan = self.plans[which]
-        offset = sum(bit for bit in plan[stage] if pattern & bit)
-        after = 0
-        if stage + 1 < len(plan):
-            after = sum(bit for bit in plan[stage + 1] if pattern & bit)
-        return stage, offset, after
 
     def copy(self, which, name):
         stage, offset, after = name
@@ -731,19 +723,30 @@
             src_ref=source.at[blocks],
             dst_ref=self.received[at].at[blocks],
             send_sem=self.send_sem.at[at],
-            recv_sem=self.recv_sem.at[which, self.pieces[which][name]],
+            recv_sem=self.recv_sem.at[which, self.pieces[which][stage, after]],
             device_id=(move(self.me, offset, self.plans[which][stage]),),
             device_id_type=MESH,
         )
 
+    def wait(self, which, stage, after):
+        plan = self.plans[which]
+        blocks = ((1 << len(plan[stage])) - 1) << len(flat(plan[stage + 2 :]))
+        at = self.wide(which, stage)
+        drain(
+            self.received[at], blocks, self.send_sem.at[at],
+            self.recv_sem.at[which, self.pieces[which][stage, after]], flip(self.me, 1),
+        ).wait_recv()
+
     def sum_of(self, which, pattern, stage):
         value = self.grads[which][self.index(which, pattern)]
         for earlier in range(stage):
+            after = 0
+            if earlier + 1 < len(self.plans[which]):
+                after = sum(bit for bit in self.plans[which][earlier + 1] if pattern & bit)
+            if (which, earlier, after) not in self.seen:
+                self.seen.add((which, earlier, after))
+                self.wait(which, earlier, after)
             for offset in subsets(self.plans[which][earlier])[1:]:
-                name = self.piece(which, earlier, pattern + offset)
-                if (which, name) not in self.seen:
-                    self.seen.add((which, name))
-                    self.copy(which, name).wait_recv()
                 slot = self.index(which, pattern + offset)
                 value = value + self.received[self.wide(which, earlier)][slot].astype(jnp.float32)
         return value
@@ -838,7 +841,7 @@
     shards, reduced, squares = refs[4:7], refs[7:10], refs[10]
     fulls, grads, received, staged = refs[11:14], refs[14:17], refs[17:23], refs[23:29]
     gather_send, gather_recv, own_squares, send_sem, recv_sem, small_send, small_recv = refs[29:36]
-    normalized, activation, hidden, block_out, log_probs = refs[36:41]
+    normalized, slopes, hidden, block_out, log_probs = refs[36:41]
     logit_grad, ff_grad, act_grad, emitted, emitted_blank = refs[41:46]
     alpha_rows, beta_rows = refs[46:50], refs[50:54]
     held, load_sem = refs[54:58], refs[58]
@@ -863,7 +866,7 @@
     pl.semaphore_wait(barrier, stage_partners(meet_plan(devices)))
     gather.pass_on()
     gather.arrive(0)
-    project_up(normalized, up_mat, activation, hidden)
+    project_up(normalized, up_mat, slopes, hidden)
     gather.arrive(1)
     gather.arrive(2)
     project_down(features, hidden, down_mat, out_mat, block_out, log_probs)
@@ -882,7 +885,7 @@
     grad_ff(logit_grad, out_mat, ff_grad)
     total.put(1, dot_first(hidden[...], ff_grad[...]))
     advance(1)
-    grad_act(ff_grad, down_mat, activation, act_grad)
+    grad_act(ff_grad, down_mat, slopes, act_grad)
     advance(1)
     total.put(0, dot_first(normalized[...], act_grad[...]))
     advance(0)

time: 48.4 us -> 44.9 us (0.928)
  Pallas kernels: 47.2 us -> 43.9 us
    pallas_call x1, Pallas kernels: 46.3 us -> 43 us  [fused_step(): pl.pallas_call(functools.partial(fused_kernel, devices, loss_scale), out_...]
where the time goes in v4:
time: 44.9 us; the launch traced here: 44.7 us
  Pallas kernels  43.9 us (98%)
  between operations  0.8 us (2%)
    pallas_call x1, Pallas kernels, fused_step(): pl.pallas_call(functools.partial(fused_kernel, devices, loss_scale), out_...  43 us

profile of v4, /device:TPU:0, one launch (start us, length us, event | category | flops | bytes accessed | tf_op | source)
XLA Modules:
  0.0 44.7 jit_solution(18093848735880550180)
XLA Ops:
  0.6 0.0 copy-start
  0.7 0.0 copy-start.1
  0.7 0.0 copy-start.2
  0.7 0.0 copy-start.3
  0.7 0.0 copy-start.4
  0.7 0.0 copy-start.5
  0.7 0.0 copy-start.6
  0.7 0.0 copy-start.7
  0.7 0.0 copy-start.8
  0.7 43.0 %fused_step.1 = (f32[64,128]{1,0:T(8,128)S(1)}, f32[64,128]{1,0:T(8,128)S(1)}, f32[16,128]{1,0:T(8,128)S(1)}, f32[32,1,128]{2,1,0:T(1,128)S(1)}) custom-call(s32[2]{0:T(128)} %refs_0_.1, s32[2]{0:T(128)} %refs_1_.1, bf16[512,256]{1,0:T(8,128)(2,1)} %bitcast.31, s32[2,48]{1,0:T(2,128)} %refs_3_.1, f32[64,128]{1,0:T(8,128)} %bitcast.19, f32[64,128]{1,0:T(8,128)} %bitcast.21, ...), custom_call_target="tpu_custom_call" | custom-call | tf_op jit(solution)/shard_map/fused_step/pallas_call | solution.py:910
  43.8 0.0 copy-done
  43.8 0.0 copy-done.1
  43.8 0.0 copy-done.2
  43.8 0.0 copy-done.3
  43.8 0.0 copy-done.4
  43.8 0.0 copy-done.5
  43.8 0.0 copy-done.6
  43.8 0.0 copy-done.7
  43.9 0.0 copy-done.8
  43.9 0.9 %adam.1 = (f32[64,128]{1,0:T(8,128)}, f32[64,128]{1,0:T(8,128)}, f32[16,128]{1,0:T(8,128)}, f32[64,128]{1,0:T(8,128)}, f32[64,128]{1,0:T(8,128)}, /*index=5*/f32...) custom-call(f32[32,1,128]{2,1,0:T(1,128)S(1)} %get-tuple-element.22.squares, ...), custom_call_target="tpu_custom_call" | custom-call | tf_op jit(solution)/shard_map/adam/pallas_call | solution.py:982
Async XLA Ops:
  0.6 43.1 %copy-start = (f32[8192]{0:T(1024)S(1)}, f32[8192]{0:T(1024)}, u32[]{:S(2)}) copy-start(f32[8192]{0:T(1024)} %param.17) | copy-start | bytes 98308
  0.7 43.1 %copy-start.1 = (f32[8192]{0:T(1024)S(1)}, f32[8192]{0:T(1024)}, u32[]{:S(2)}) copy-start(f32[8192]{0:T(1024)} %param.18) | copy-start | bytes 98308
  0.7 43.1 %copy-start.2 = (f32[8192]{0:T(1024)S(1)}, f32[8192]{0:T(1024)}, u32[]{:S(2)}) copy-start(f32[8192]{0:T(1024)} %param.20) | copy-start | bytes 98308
  0.7 43.1 %copy-start.3 = (f32[8192]{0:T(1024)S(1)}, f32[8192]{0:T(1024)}, u32[]{:S(2)}) copy-start(f32[8192]{0:T(1024)} %param.21) | copy-start | bytes 98308
  0.7 43.1 %copy-start.4 = (f32[8192]{0:T(1024)S(1)}, f32[8192]{0:T(1024)}, u32[]{:S(2)}) copy-start(f32[8192]{0:T(1024)} %param.23) | copy-start | bytes 98308
  0.7 43.1 %copy-start.5 = (f32[8192]{0:T(1024)S(1)}, f32[8192]{0:T(1024)}, u32[]{:S(2)}) copy-start(f32[8192]{0:T(1024)} %param.24) | copy-start | bytes 98308
  0.7 43.1 %copy-start.6 = (f32[2048]{0:T(1024)S(1)}, f32[2048]{0:T(1024)}, u32[]{:S(2)}) copy-start(f32[2048]{0:T(1024)} %param.19) | copy-start | bytes 24580
  0.7 43.1 %copy-start.7 = (f32[2048]{0:T(1024)S(1)}, f32[2048]{0:T(1024)}, u32[]{:S(2)}) copy-start(f32[2048]{0:T(1024)} %param.22) | copy-start | bytes 24580
  0.7 43.1 %copy-start.8 = (f32[2048]{0:T(1024)S(1)}, f32[2048]{0:T(1024)}, u32[]{:S(2)}) copy-start(f32[2048]{0:T(1024)} %param.25) | copy-start | bytes 24580

commit v5 on v4

--- a/solution.py
+++ b/solution.py
@@ -325,8 +325,8 @@
 
 
 def ctc_rows(frames):
-    return [pltpu.VMEM((frames, 8, LANES), jnp.float32)] * 4 + [
-        pltpu.VMEM((2 * frames, 8, LANES), jnp.float32)
+    return [pltpu.VMEM((8 * frames, LANES), jnp.float32)] * 4 + [
+        pltpu.VMEM((16 * frames, LANES), jnp.float32)
     ] * 4
 
 
@@ -347,8 +347,13 @@
             return jnp.broadcast_to(values[self.row : self.row + 1], (8, LANES))
 
         blank, label = whole(blank), whole(label)
-        self.blank = [self.spread(blank, part) for part in range(self.parts)]
-        self.label = [self.spread(label, part) for part in range(self.parts + 1)]
+        return tuple(
+            [self.spread(blank, part) for part in range(self.parts)]
+            + [self.spread(label, part) for part in range(self.parts + 1)]
+        )
+
+    def enter(self, moved):
+        self.blank, self.label = list(moved[: self.parts]), list(moved[self.parts :])
         one = jnp.ones((8, LANES), jnp.float32)
         self.blank_mass, self.label_mass = [one] * self.parts, [one] * (self.parts + 1)
 
@@ -451,47 +456,61 @@
         )
     nothing = jnp.full((8, LANES), negative, jnp.float32)
 
+    def tile(frame):
+        return pl.ds(pl.multiple_of(frame * 8, 8), 8)
+
     def row_of(ref, frame):
         return jnp.broadcast_to(ref[pl.ds(frame, 1), :], (8, LANES))
 
+    def leave(lattice):
+        return (
+            lattice.blank[0] + jnp.log2(lattice.blank_mass[0]),
+            lattice.label[0] + jnp.log2(lattice.label_mass[0]),
+        )
+
+    def step_back(at, level):
+        frame = at * depth + level
+        emit = emit_blank = None
+        for utterance in range(utterances):
+            back = jnp.maximum(frame_lens[utterance] - 1 - frame, 0)
+            mine, mine_blank = row_of(emitted, back), row_of(emitted_blank, back)
+            if utterance == 0:
+                emit, emit_blank = mine, mine_blank
+            else:
+                emit = jnp.where(lane_row < half * utterance, emit, mine)
+                emit_blank = jnp.where(lane_row < half * utterance, emit_blank, mine_blank)
+        result = backward.advance(emit_blank, emit, min(PARTS, depth - level))
+        for ref, value in zip(beta_rows, result):
+            ref[tile(frames - 1 - frame), :] = value
+
+    def step_ahead(at, level):
+        frame = at * depth + level
+        result = forward.advance(
+            row_of(emitted_blank, frame), row_of(emitted, frame), min(PARTS, depth - level)
+        )
+        for ref, value in zip(alpha_rows, result):
+            ref[tile(frame), :] = value
+
     def block(at, carry):
-        forward.begin(*carry[:2])
-        backward.begin(*carry[2:])
+        forward.enter(forward.begin(*carry[:2]))
+        backward.enter(backward.begin(*carry[2:]))
         for level in range(depth):
-            frame = at * depth + level
-            needed = min(PARTS, depth - level)
-            result = forward.advance(row_of(emitted_blank, frame), row_of(emitted, frame), needed)
-            for ref, value in zip(alpha_rows, result):
-                ref[frame] = value
-            emit = emit_blank = None
-            for utterance in range(utterances):
-                back = jnp.maximum(frame_lens[utterance] - 1 - frame, 0)
-                mine, mine_blank = row_of(emitted, back), row_of(emitted_blank, back)
-                if utterance == 0:
-                    emit, emit_blank = mine, mine_blank
-                else:
-                    emit = jnp.where(lane_row < half * utterance, emit, mine)
-                    emit_blank = jnp.where(lane_row < half * utterance, emit_blank, mine_blank)
-            result = backward.advance(emit_blank, emit, needed)
-            for ref, value in zip(beta_rows, result):
-                ref[frames - 1 - frame] = value
-        return tuple(
-            values[0] + jnp.log2(mass[0])
-            for lattice in (forward, backward)
-            for values, mass in (
-                (lattice.blank, lattice.blank_mass), (lattice.label, lattice.label_mass)
-            )
-        )
-
-    lax.fori_loop(0, frames // depth, block, (start, nothing, start_back, nothing))
+            step_ahead(at, level)
+            step_back(at, level)
+        return leave(forward) + leave(backward)
+
+    lax.fori_loop(
+        0, frames // depth, block, (start, nothing, start_back, nothing)
+    )
 
     frame_ids = lax.broadcasted_iota(jnp.int32, (frames, LANES), 0)
-    alphas = [ref[:, forward.row, :] for ref in alpha_rows]
+    alphas = [ref[pl.ds(forward.row, frames, stride=8), :] for ref in alpha_rows]
     betas, alive = [], None
     for ref in beta_rows:
         value = None
         for utterance in range(utterances):
-            mine = ref[pl.ds(frames - frame_lens[utterance], frames), backward.row, :]
+            first = 8 * (frames - frame_lens[utterance]) + backward.row
+            mine = ref[pl.ds(first, frames, stride=8), :]
             value = mine if value is None else jnp.where(frame_lanes < half * utterance, value, mine)
         betas.append(value)
     betas[0], betas[1] = pltpu.roll(betas[0], 1, 1), pltpu.roll(betas[1], 1, 1)
@@ -688,6 +707,12 @@
     return pieces
 
 
+def far_first(offset, bits):
+    core, near, far = bits[:1], bits[1:3], bits[3:]
+    weights = [1] * len(core) + [3] * len(near) + [3 << at for at in range(len(far))]
+    return sum(weight for weight, bit in zip(weights, bits) if offset & bit)
+
+
 class StagedSum:
     def __init__(self, me, plans, narrow, grads, received, staged, send_sem, recv_sem):
         self.me, self.plans, self.narrow = me, plans, narrow
@@ -779,14 +804,14 @@
         own_squares[...] = own
         squares[0] = own
 
-        @pl.loop(1, devices)
-        def _(shift):
+        bits = [1 << k for k in range(devices.bit_length() - 1)]
+        for offset in sorted(subsets(bits)[1:], key=lambda at: -far_first(at, bits)):
             pltpu.make_async_remote_copy(
                 src_ref=own_squares,
-                dst_ref=squares.at[shift],
+                dst_ref=squares.at[offset],
                 send_sem=small_send,
                 recv_sem=small_recv,
-                device_id=((me + shift) % devices,),
+                device_id=(move(me, offset, bits),),
                 device_id_type=MESH,
             ).start()
 
@@ -887,12 +912,11 @@
     advance(1)
     grad_act(ff_grad, down_mat, slopes, act_grad)
     advance(1)
+    total.put(2, dot_first(block_out[...], logit_grad[...]))
+    advance(2)
     total.put(0, dot_first(normalized[...], act_grad[...]))
     advance(0)
-    total.put(2, dot_first(block_out[...], logit_grad[...]))
-    advance(2)
-    while any(pending):
-        advance(1, 0, 2)
+    advance(2, 0, 1, 0, 2)
     total.finish(devices, reduced, squares, own_squares, small_send, small_recv)
     gather.close()
 

time: 44.9 us -> 42.1 us (0.938)
  Pallas kernels: 43.9 us -> 41.1 us
    pallas_call x1, Pallas kernels: 43 us -> 40.2 us  [fused_step(): pl.pallas_call(functools.partial(fused_kernel, devices, loss_scale), out_...]
where the time goes in v5:
time: 42.1 us; the launch traced here: 41.9 us
  Pallas kernels  41.1 us (98%)
  between operations  0.8 us (2%)
    pallas_call x1, Pallas kernels, fused_step(): pl.pallas_call(functools.partial(fused_kernel, devices, loss_scale), out_...  40.2 us
    pallas_call x1, Pallas kernels, adam(): pl.pallas_call(adam_kernel, out_shape=shapes * 3, in_specs=[VMEM] * 13, o...  0.87 us

profile of v5, /device:TPU:0, one launch (start us, length us, event | category | flops | bytes accessed | tf_op | source)
XLA Modules:
  0.0 41.9 jit_solution(1338136565384686874)
XLA Ops:
  0.6 0.0 copy-start
  0.7 0.0 copy-start.1
  0.7 0.0 copy-start.2
  0.7 0.0 copy-start.3
  0.7 0.0 copy-start.4
  0.7 0.0 copy-start.5
  0.7 0.0 copy-start.6
  0.7 0.0 copy-start.7
  0.7 0.0 copy-start.8
  0.7 40.2 %fused_step.1 = (f32[64,128]{1,0:T(8,128)S(1)}, f32[64,128]{1,0:T(8,128)S(1)}, f32[16,128]{1,0:T(8,128)S(1)}, f32[32,1,128]{2,1,0:T(1,128)S(1)}) custom-call(s32[2]{0:T(128)} %refs_0_.1, s32[2]{0:T(128)} %refs_1_.1, bf16[512,256]{1,0:T(8,128)(2,1)} %bitcast.31, s32[2,48]{1,0:T(2,128)} %refs_3_.1, f32[64,128]{1,0:T(8,128)} %bitcast.19, f32[64,128]{1,0:T(8,128)} %bitcast.21, ...), custom_call_target="tpu_custom_call" | custom-call | tf_op jit(solution)/shard_map/fused_step/pallas_call | solution.py:934
  41.0 0.0 copy-done
  41.0 0.0 copy-done.1
  41.0 0.0 copy-done.2
  41.0 0.0 copy-done.3
  41.0 0.0 copy-done.4
  41.0 0.0 copy-done.5
  41.0 0.0 copy-done.6
  41.0 0.0 copy-done.7
  41.0 0.0 copy-done.8
  41.1 0.9 %adam.1 = (f32[64,128]{1,0:T(8,128)}, f32[64,128]{1,0:T(8,128)}, f32[16,128]{1,0:T(8,128)}, f32[64,128]{1,0:T(8,128)}, f32[64,128]{1,0:T(8,128)}, /*index=5*/f32...) custom-call(f32[32,1,128]{2,1,0:T(1,128)S(1)} %get-tuple-element.22.squares, ...), custom_call_target="tpu_custom_call" | custom-call | tf_op jit(solution)/shard_map/adam/pallas_call | solution.py:1006
Async XLA Ops:
  0.6 40.3 %copy-start = (f32[8192]{0:T(1024)S(1)}, f32[8192]{0:T(1024)}, u32[]{:S(2)}) copy-start(f32[8192]{0:T(1024)} %param.17) | copy-start | bytes 98308
  0.7 40.3 %copy-start.1 = (f32[8192]{0:T(1024)S(1)}, f32[8192]{0:T(1024)}, u32[]{:S(2)}) copy-start(f32[8192]{0:T(1024)} %param.18) | copy-start | bytes 98308
  0.7 40.3 %copy-start.2 = (f32[8192]{0:T(1024)S(1)}, f32[8192]{0:T(1024)}, u32[]{:S(2)}) copy-start(f32[8192]{0:T(1024)} %param.20) | copy-start | bytes 98308
  0.7 40.3 %copy-start.3 = (f32[8192]{0:T(1024)S(1)}, f32[8192]{0:T(1024)}, u32[]{:S(2)}) copy-start(f32[8192]{0:T(1024)} %param.21) | copy-start | bytes 98308
  0.7 40.3 %copy-start.4 = (f32[8192]{0:T(1024)S(1)}, f32[8192]{0:T(1024)}, u32[]{:S(2)}) copy-start(f32[8192]{0:T(1024)} %param.23) | copy-start | bytes 98308
  0.7 40.3 %copy-start.5 = (f32[8192]{0:T(1024)S(1)}, f32[8192]{0:T(1024)}, u32[]{:S(2)}) copy-start(f32[8192]{0:T(1024)} %param.24) | copy-start | bytes 98308
  0.7 40.3 %copy-start.6 = (f32[2048]{0:T(1024)S(1)}, f32[2048]{0:T(1024)}, u32[]{:S(2)}) copy-start(f32[2048]{0:T(1024)} %param.19) | copy-start | bytes 24580
  0.7 40.3 %copy-start.7 = (f32[2048]{0:T(1024)S(1)}, f32[2048]{0:T(1024)}, u32[]{:S(2)}) copy-start(f32[2048]{0:T(1024)} %param.22) | copy-start | bytes 24580
  0.7 40.3 %copy-start.8 = (f32[2048]{0:T(1024)S(1)}, f32[2048]{0:T(1024)}, u32[]{:S(2)}) copy-start(f32[2048]{0:T(1024)} %param.25) | copy-start | bytes 24580

commit v6 on v5

--- a/solution.py
+++ b/solution.py
@@ -141,10 +141,10 @@
                     pl.ds(part, rows, stride=parts), :
                 ].astype(jnp.bfloat16)
 
-    def send(self, which, source, first):
+    def send(self, which, source, first, end=None):
         plan, full = self.plans[which], self.fulls[which]
         units, sems, _ = self.units[which]
-        for stage in range(first, len(plan)):
+        for stage in range(first, end or len(plan)):
             for offset in subsets(plan[stage])[1:][::-1]:
                 peer = move(self.me, offset, plan[stage])
                 for pattern in units[source][0] if source else [0]:
@@ -165,8 +165,9 @@
         )
 
     def pass_on(self):
-        for which in range(3):
-            self.send(which, None, 0)
+        for stage in range(max(len(plan) for plan in self.plans)):
+            for which in range(3):
+                self.send(which, None, stage, stage + 1)
         names = [list(units[0]) for units in self.units]
         for at in range(max(len(some) for some in names)):
             for which in range(3):
@@ -792,15 +793,17 @@
 
     def finish(self, devices, reduced, squares, own_squares, small_send, small_recv):
         me = self.me
-        own = jnp.zeros((1, LANES), jnp.float32)
+        own = jnp.zeros((8, LANES), jnp.float32)
+        values = {}
         for which in (2, 1, 0):
             value = self.sum_of(which, 0, len(self.plans[which]))
+            values[which] = value
             rows, width = value.shape
-            parts = width // LANES
-            for part in range(parts):
-                piece = value[:, part * LANES : (part + 1) * LANES]
-                reduced[which][pl.ds(part, rows, stride=parts), :] = piece
-                own = own + jnp.sum(piece * piece, axis=0, keepdims=True)
+            for row in range(0, rows, 8):
+                for lane in range(0, width, LANES):
+                    piece = value[row : row + 8, lane : lane + LANES]
+                    own = own + piece * piece
+        own = jnp.sum(own, axis=0, keepdims=True)
         own_squares[...] = own
         squares[0] = own
 
@@ -814,6 +817,14 @@
                 device_id=(move(me, offset, bits),),
                 device_id_type=MESH,
             ).start()
+
+        for which, value in values.items():
+            rows, width = value.shape
+            parts = width // LANES
+            for part in range(parts):
+                reduced[which][pl.ds(part, rows, stride=parts), :] = value[
+                    :, part * LANES : (part + 1) * LANES
+                ]
 
         for which, plan in enumerate(self.plans):
             sent = {}

time: 42.1 us -> 42 us (level)
  no operation moved by 1% of the time
where the time goes in v6:
time: 42 us; the launch traced here: 41.8 us
  Pallas kernels  40.9 us (97%)
  between operations  0.8 us (2%)
    pallas_call x1, Pallas kernels, fused_step(): pl.pallas_call(functools.partial(fused_kernel, devices, loss_scale), out_...  40.1 us
    pallas_call x1, Pallas kernels, adam(): pl.pallas_call(adam_kernel, out_shape=shapes * 3, in_specs=[VMEM] * 13, o...  0.87 us

profile of v6, /device:TPU:0, one launch (start us, length us, event | category | flops | bytes accessed | tf_op | source)
XLA Modules:
  0.0 41.8 jit_solution(10940934209369600035)
XLA Ops:
  0.6 0.0 copy-start
  0.7 0.0 copy-start.1
  0.7 0.0 copy-start.2
  0.7 0.0 copy-start.3
  0.7 0.0 copy-start.4
  0.7 0.0 copy-start.5
  0.7 0.0 copy-start.6
  0.7 0.0 copy-start.7
  0.7 0.0 copy-start.8
  0.7 40.1 %fused_step.1 = (f32[64,128]{1,0:T(8,128)S(1)}, f32[64,128]{1,0:T(8,128)S(1)}, f32[16,128]{1,0:T(8,128)S(1)}, f32[32,1,128]{2,1,0:T(1,128)S(1)}) custom-call(s32[2]{0:T(128)} %refs_0_.1, s32[2]{0:T(128)} %refs_1_.1, bf16[512,256]{1,0:T(8,128)(2,1)} %bitcast.31, s32[2,48]{1,0:T(2,128)} %refs_3_.1, f32[64,128]{1,0:T(8,128)} %bitcast.19, f32[64,128]{1,0:T(8,128)} %bitcast.21, ...), custom_call_target="tpu_custom_call" | custom-call | tf_op jit(solution)/shard_map/fused_step/pallas_call | solution.py:945
  40.8 0.0 copy-done
  40.8 0.0 copy-done.1
  40.8 0.0 copy-done.2
  40.8 0.0 copy-done.3
  40.8 0.0 copy-done.4
  40.8 0.0 copy-done.5
  40.9 0.0 copy-done.6
  40.9 0.0 copy-done.7
  40.9 0.0 copy-done.8
  40.9 0.9 %adam.1 = (f32[64,128]{1,0:T(8,128)}, f32[64,128]{1,0:T(8,128)}, f32[16,128]{1,0:T(8,128)}, f32[64,128]{1,0:T(8,128)}, f32[64,128]{1,0:T(8,128)}, /*index=5*/f32...) custom-call(f32[32,1,128]{2,1,0:T(1,128)S(1)} %get-tuple-element.22.squares, ...), custom_call_target="tpu_custom_call" | custom-call | tf_op jit(solution)/shard_map/adam/pallas_call | solution.py:1017
Async XLA Ops:
  0.6 40.2 %copy-start = (f32[8192]{0:T(1024)S(1)}, f32[8192]{0:T(1024)}, u32[]{:S(2)}) copy-start(f32[8192]{0:T(1024)} %param.17) | copy-start | bytes 98308
  0.7 40.2 %copy-start.1 = (f32[8192]{0:T(1024)S(1)}, f32[8192]{0:T(1024)}, u32[]{:S(2)}) copy-start(f32[8192]{0:T(1024)} %param.18) | copy-start | bytes 98308
  0.7 40.2 %copy-start.2 = (f32[8192]{0:T(1024)S(1)}, f32[8192]{0:T(1024)}, u32[]{:S(2)}) copy-start(f32[8192]{0:T(1024)} %param.20) | copy-start | bytes 98308
  0.7 40.2 %copy-start.3 = (f32[8192]{0:T(1024)S(1)}, f32[8192]{0:T(1024)}, u32[]{:S(2)}) copy-start(f32[8192]{0:T(1024)} %param.21) | copy-start | bytes 98308
  0.7 40.2 %copy-start.4 = (f32[8192]{0:T(1024)S(1)}, f32[8192]{0:T(1024)}, u32[]{:S(2)}) copy-start(f32[8192]{0:T(1024)} %param.23) | copy-start | bytes 98308
  0.7 40.2 %copy-start.5 = (f32[8192]{0:T(1024)S(1)}, f32[8192]{0:T(1024)}, u32[]{:S(2)}) copy-start(f32[8192]{0:T(1024)} %param.24) | copy-start | bytes 98308
  0.7 40.2 %copy-start.6 = (f32[2048]{0:T(1024)S(1)}, f32[2048]{0:T(1024)}, u32[]{:S(2)}) copy-start(f32[2048]{0:T(1024)} %param.19) | copy-start | bytes 24580
  0.7 40.2 %copy-start.7 = (f32[2048]{0:T(1024)S(1)}, f32[2048]{0:T(1024)}, u32[]{:S(2)}) copy-start(f32[2048]{0:T(1024)} %param.22) | copy-start | bytes 24580
  0.7 40.2 %copy-start.8 = (f32[2048]{0:T(1024)S(1)}, f32[2048]{0:T(1024)}, u32[]{:S(2)}) copy-start(f32[2048]{0:T(1024)} %param.25) | copy-start | bytes 24580
